TPU v7x, 8 devices: a whole 2x2x1 slice. The times are simulated.
8 devices in a mesh: sys: 1 (over z), aux: 2 (over y), orb: 4 (over x, core).
Axes of the slice: x: 2, y: 2, z: 1, core: 2. Of those that a mesh axis runs over, the one named last changes fastest.
Arguments:
- aux_ints: float32 [928, 464, 464], P(('sys', 'aux'), 'orb')
- metric: float32 [928, 928], P(('sys', 'aux'))
- orbitals: float32 [1, 464, 40], P('sys')
Outputs:
- output: float32 [1, 464, 464], P('sys', 'orb', 'aux')
All inputs are finite; a program needn't handle non-finite values.
Results may differ from a plain program's by a relative error of at most 0.001.
Values are sent between devices in bfloat16 or wider.
A program may use at most 1 GiB of HBM per device.

v0:
```python
import jax
import jax.numpy as jnp
from jax import lax
from jax.sharding import PartitionSpec as P

PRECISE = lax.Precision.HIGHEST


def solution(mesh):
    def local_fock(ints_blk, metric_blk, orbitals):
        m_loc = ints_blk.shape[1]
        row_start = lax.axis_index('orb') * m_loc
        half_tr = jnp.einsum('qml,dli->qmdi', ints_blk, orbitals, precision=PRECISE, preferred_element_type=jnp.float32)
        orb_rows = lax.dynamic_slice_in_dim(orbitals, row_start, m_loc, axis=1)
        gamma_part = jnp.einsum('qmdi,dmi->dq', half_tr, orb_rows, precision=PRECISE, preferred_element_type=jnp.float32)
        gamma_raw = lax.psum(gamma_part, 'orb')
        gamma_all = lax.all_gather(gamma_raw, 'aux', axis=1, tiled=True)
        gamma_fit = jnp.einsum('dq,pq->dp', gamma_all, metric_blk, precision=PRECISE, preferred_element_type=jnp.float32)
        weight_part = jnp.dot(gamma_fit, metric_blk, precision=PRECISE, preferred_element_type=jnp.float32)
        weights = lax.psum_scatter(weight_part, 'aux', scatter_dimension=1, tiled=True)
        coulomb = jnp.einsum('dq,qmn->dmn', weights, ints_blk, precision=PRECISE, preferred_element_type=jnp.float32)
        half_all = lax.all_gather(half_tr, 'aux', axis=0, tiled=True)
        fitted = jnp.einsum('pq,qmdi->pmdi', metric_blk, half_all, precision=PRECISE, preferred_element_type=jnp.float32)
        fitted_all = lax.all_gather(fitted, 'orb', axis=1, tiled=True)
        exchange = jnp.einsum('pmdi,pndi->dmn', fitted, fitted_all, precision=PRECISE, preferred_element_type=jnp.float32)
        fock_part = 2.0 * coulomb - exchange
        return lax.psum_scatter(fock_part, 'aux', scatter_dimension=2, tiled=True)

    return jax.shard_map(local_fock, mesh=mesh, in_specs=(P(('sys', 'aux'), 'orb', None), P(('sys', 'aux'), None), P('sys', None, None)), out_specs=P('sys', 'orb', 'aux'), check_vma=False)
```

profile of v0, /device:TPU:0, one launch (start us, length us, event | category | flops | bytes accessed | tf_op | source)
XLA Modules:
  0.0 708.0 jit_solution(5925713668362937354)
XLA Ops:
  6.5 0.0 copy-start
  6.5 0.0 all-gather.5.cloned.1.call-start
  6.5 102.5 %fusion.26 = f32[464,116,40]{0,2,1:T(8,128)} fusion(f32[464,116,464]{2,0,1:T(8,128)} %param.3, f32[1,464,40]{1,2,0:T(8,128)} %param.5), kind=kOutput, calls=%fused_computation.16 | convolution fusion | flops 11987681280 | bytes 108583424 | tf_op jit(solution)/shard_map/qml,dli->qmdi/dot_general | solution.py:13
  109.0 0.0 copy-start.2
  109.0 11.8 %copy.15 = f32[464,116,40]{1,2,0:T(8,128)} copy(f32[464,116,40]{0,2,1:T(8,128)} %fusion.26) | data formatting | bytes 17223680 | tf_op jit(solution)/shard_map/qml,dli->qmdi/dot_general | solution.py:13
  120.8 0.0 all-gather.5.cloned.1.call-update
  120.9 0.0 reduce-scatter.8.cloned.1.call-start
  120.9 0.0 copy-done.2
  120.9 0.6 dynamic-slice
  122.2 0.9 constant_dynamic-slice_fusion
  123.0 10.9 %fusion.21 = f32[1,464]{1,0:T(1,128)S(1)} fusion(f32[116,40,1]{0,2,1:T(1,128)S(1)} %bitcast.59, f32[464,116,40]{0,2,1:T(8,128)} %fusion.26), kind=kOutput, calls=%fused_computation.11 | convolution fusion | flops 25835520 | bytes 8632256 | tf_op jit(solution)/shard_map/qmdi,dmi->dq/dot_general | solution.py:15
  133.9 8.7 %psum.7 = f32[1,464]{1,0:T(1,128)S(1)} all-reduce(f32[1,464]{1,0:T(1,128)S(1)} %fusion.21), channel_id=1, replica_groups=mesh['sys'=1,'aux'=2,'orb'=4] {'orb'}, use_global_device_ids=true, to_apply=%region_0.0 | all-reduce | flops 464 | bytes 3712 | tf_op jit(solution)/shard_map/psum | solution.py:16
  142.7 0.2 dynamic-update-slice
  142.9 18.1 %all-reduce = f32[928]{0:T(1024)S(1)} all-reduce(f32[928]{0:T(1024)S(1)} %dynamic-update-slice), channel_id=1, replica_groups=mesh['sys'=1,'aux'=2,'orb'=4] {'aux'}, use_global_device_ids=true, to_apply=%add | all-reduce | flops 928 | bytes 7424 | tf_op jit(solution)/shard_map/reshape.5
  161.0 0.0 copy-done
  161.0 1.6 convolution_bitcast_fusion.2
  162.7 4.2 convolution_bitcast_fusion.1
  166.9 0.0 reduce-scatter.8.cloned.1.call-update
  166.9 0.0 all-gather.7.cloned.1.call-start
  167.0 180.4 %all-gather.5.cloned.1.call-done = f32[928,116,40]{1,2,0:T(8,128)} async-done(((f32[464,116,40]{1,2,0:T(8,128)}), f32[928,116,40]{1,2,0:T(8,128)}) %all-gather.5.cloned.1.call-update) | async-done | bytes 17223696 | tf_op jit(solution)/shard_map/all_gather | solution.py:22
  347.3 19.7 %copy.10 = f32[928,116,40]{0,2,1:T(8,128)} copy(f32[928,116,40]{1,2,0:T(8,128)} %all-gather.5.cloned.1.call-done) | data formatting | bytes 34447360 | tf_op jit(solution)/shard_map/all_gather | solution.py:22
  367.1 34.3 %convolution_bitcast_fusion = f32[464,116,40]{0,2,1:T(8,128)} fusion(f32[928,116,40]{0,2,1:T(8,128)} %copy.10, f32[464,928]{1,0:T(8,128)S(1)} %copy-done), kind=kOutput, calls=%fused_computation.5 | convolution fusion | flops 23975362560 | bytes 27557888 | tf_op jit(solution)/shard_map/pq,qmdi->pmdi/dot_general | solution.py:23
  401.4 0.0 all-gather.7.cloned.1.call-update
  401.4 0.0 reduce-scatter.10.cloned.1.call-start
  401.5 0.0 reduce-scatter.8.cloned.1.call-done
  401.5 55.9 %fusion.24 = f32[1,116,464]{2,0,1:T(1,128)S(1)} fusion(f32[464,116,464]{2,0,1:T(8,128)} %param.3, f32[464,1]{1,0:T(8,128)} %reduce-scatter.8.cloned.1.call-done), kind=kOutput, calls=%fused_computation.13 | convolution fusion | flops 299692032 | bytes 100114496 | tf_op jit(solution)/shard_map/dq,qmn->dmn/dot_general | solution.py:21
  457.4 0.1 copy.18
  457.6 170.3 %all-gather.7.cloned.1.call-done = f32[464,464,40]{0,2,1:T(8,128)} async-done(((f32[464,116,40]{0,2,1:T(8,128)}), f32[464,464,40]{0,2,1:T(8,128)}) %all-gather.7.cloned.1.call-update) | async-done | bytes 34447376 | tf_op jit(solution)/shard_map/all_gather | solution.py:24
  627.9 0.0 copy-start.1
  627.9 62.7 %fusion.16 = f32[1,116,464]{1,2,0:T(8,128)} fusion(f32[464,464,40]{0,2,1:T(8,128)} %all-gather.7.cloned.1.call-done, f32[464,116,40]{0,2,1:T(8,128)} %convolution_bitcast_fusion, f32[1,116,464]{1,2,0:T(8,128)S(1)} %copy.18), kind=kOutput, calls=%fused_computation.10 | convolution fusion | flops 11987788800 | bytes 43489792 | tf_op jit(solution)/shard_map/pmdi,pndi->dmn/dot_general | solution.py:25
  690.6 0.0 reduce-scatter.10.cloned.1.call-update
  690.6 8.8 %reduce-scatter.10.cloned.1.call-done = f32[1,116,232]{1,2,0:T(8,128)} async-done(((f32[1,116,464]{1,2,0:T(8,128)}), f32[1,116,232]{1,2,0:T(8,128)}) %reduce-scatter.10.cloned.1.call-update) | async-done | bytes 107664
  699.4 1.7 copy.13
  701.0 0.0 copy-done.1
  (1 shorter events, 0.0 us)
Async XLA Ops:
  6.5 154.5 %copy-start = (f32[464,928]{1,0:T(8,128)S(1)}, f32[464,928]{1,0:T(8,128)}, u32[]{:S(2)}) copy-start(f32[464,928]{1,0:T(8,128)} %param.4) | copy-start | bytes 5167108
  6.5 340.8 %all-gather.5.cloned.1.call-start = ((), (), s32[]{:S(2)}) async-start(), calls=%async_computation.2 | async-start | bytes 28508160 | tf_op jit(solution)/shard_map/all_gather | solution.py:22
  109.0 11.9 %copy-start.2 = (u32[8]{0:T(128)S(1)}, u32[8]{0:T(128)}, u32[]{:S(2)}) copy-start(u32[8]{0:T(128)} %constant.14) | copy-start | bytes 100
  120.9 280.6 %reduce-scatter.8.cloned.1.call-start = ((), (), s32[]{:S(2)}) async-start(), calls=%async_computation.4 | async-start | bytes 712704
  166.9 460.9 %all-gather.7.cloned.1.call-start = ((), (), s32[]{:S(2)}) async-start(), calls=%async_computation.3 | async-start | bytes 47513600 | tf_op jit(solution)/shard_map/all_gather | solution.py:24
  401.4 298.0 %reduce-scatter.10.cloned.1.call-start = ((), (), s32[]{:S(2)}) async-start(), calls=%async_computation.5 | async-start | bytes 356352
  627.9 73.2 %copy-start.1 = (f32[464,928]{1,0:T(8,128)S(1)}, f32[464,928]{1,0:T(8,128)}, u32[]{:S(2)}) copy-start(f32[464,928]{1,0:T(8,128)} %param.4) | copy-start | bytes 5167108
Sparse Core Ops, SparseCore 0:
  121.0 226.3 all-gather.4
  349.6 11.1 reduce-scatter.7
  401.5 226.2 all-gather.6
  690.7 8.6 reduce-scatter.9
where the time goes:
time: 721 us; the launch traced here: 708 us
  waiting for transfers between devices  359 us (50%)
  matrix products  272 us (38%)
  local copies, waits for them, and re-layouts  35 us (5%)
  blocking collectives  26.8 us (4%)
  between operations  14.2 us (2%)
    all_gather x1, waiting for transfers between devices, local_fock(): half_all = lax.all_gather(half_tr, 'aux', axis=0, tiled=True)  180 us
    all_gather x1, waiting for transfers between devices, local_fock(): fitted_all = lax.all_gather(fitted, 'orb', axis=1, tiled=True)  170 us
    dot_general x1, matrix products, local_fock(): jnp.einsum('qml,dli->qmdi', ints_blk, orbitals, precision=PRECISE, prefer...  102 us
    dot_general x1, matrix products, local_fock(): jnp.einsum('pmdi,pndi->dmn', fitted, fitted_all, precision=PRECISE, prefe...  62.7 us
    dot_general x1, matrix products, local_fock(): jnp.einsum('dq,qmn->dmn', weights, ints_blk, precision=PRECISE, preferred...  55.9 us
    dot_general x1, matrix products, local_fock(): jnp.einsum('pq,qmdi->pmdi', metric_blk, half_all, precision=PRECISE, pref...  34.3 us
    all_gather x1, local copies, waits for them, and re-layouts, local_fock(): half_all = lax.all_gather(half_tr, 'aux', axis=0, tiled=True)  19.7 us
    another operation x1, blocking collectives  18.1 us
  transfers between devices with their start and end apart: 4, of which 3 were waited for; matrix products, arithmetic and copies ran while one was open for 18% of the time, Pallas kernels for 0%

commit v1 on v0

v1 whole, which is shorter than its diff:
```python
import jax
import jax.numpy as jnp
from jax import lax
from jax.experimental import pallas as pl
from jax.experimental.pallas import tpu as pltpu

P = jax.sharding.PartitionSpec
F32, BF16 = jnp.float32, jnp.bfloat16
MESH = pl.DeviceIdType.MESH
NT = (((1,), (1,)), ((), ()))

NAUX, NORB, NDEV = 2, 4, 8
QB, MB, NB, NI = 464, 116, 464, 40
IV = NI // NDEV
QP, MP = 512, 120
MC = 8
NCH = MP // MC
TAIL = MB - MC * (NCH - 1)
SP = 48
NBUF = 12
NSP = 4


def split3(x):
    a = x.astype(BF16)
    r = x - a.astype(F32)
    b = r.astype(BF16)
    c = (r - b.astype(F32)).astype(BF16)
    return a, b, c


def half_kernel(b_hbm, ct_ref, co_ref, md_hbm, arecv, grecv, mrecv,
                bbuf, bs, cw, abuf, sbuf, gbuf, gsend,
                bsem, ssem, rsem, osem, gs_sem, gr_sem, ms_sem, mr_sem):
    aux, orb = lax.axis_index('aux'), lax.axis_index('orb')
    me = aux * NORB + orb

    def at(d):
        return {'aux': d // NORB, 'orb': lax.rem(d, NORB)}

    def peer(t):
        return lax.rem(me + t, NDEV)

    def fetch(m, slot):
        return pltpu.make_async_copy(b_hbm.at[m], bbuf.at[slot], bsem.at[slot])

    for m in range(NBUF):
        fetch(m, m).start()

    barrier = pltpu.get_barrier_semaphore()
    for t in range(1, NDEV):
        pl.semaphore_signal(barrier, inc=1, device_id=at(peer(t)), device_id_type=MESH)

    abuf[...] = jnp.zeros_like(abuf)
    gbuf[...] = jnp.zeros_like(gbuf)
    c1, c2, c3 = split3(ct_ref[...])
    cw[...] = jnp.concatenate(
        [c1.astype(F32), c2.astype(F32), c3.astype(F32), jnp.zeros((8, NB), F32)], axis=0).astype(BF16)

    pl.semaphore_wait(barrier, NDEV - 1)
    mcopy = pltpu.make_async_remote_copy(md_hbm, mrecv, ms_sem, mr_sem,
                                         device_id={'aux': 1 - aux, 'orb': orb}, device_id_type=MESH)
    mcopy.start()

    def place(c):
        return arecv.at[aux, :, pl.ds(pl.multiple_of(orb * MP + c * MC, 8), MC), :]

    def send(c, slot, t):
        d = peer(t)
        return pltpu.make_async_remote_copy(sbuf.at[slot, d], place(c), ssem.at[slot, t], rsem.at[t],
                                            device_id=at(d), device_id_type=MESH)

    def own(c, slot):
        return pltpu.make_async_copy(sbuf.at[slot, me], place(c), osem.at[slot])

    def chunk(c, rows, more):
        two = lax.rem(c, 2)
        for k in range(rows):
            m = c * MC + k
            slot = lax.rem(m, NBUF)
            fetch(m, slot).wait()
            parts = split3(bbuf[slot])
            r = None
            for j in range(3):
                bs[k % NSP, j] = parts[j]
            for j in range(3):
                x = lax.dot_general(cw[...], bs[k % NSP, j], NT, preferred_element_type=F32)
                r = x if r is None else r + x
            a2 = r[0:NI] + r[NI:2 * NI] + r[2 * NI:3 * NI]
            for v in range(IV):
                for lt in range(4):
                    l0, l1 = lt * 128, min(lt * 128 + 128, QB)
                    abuf[lt, pl.ds(v * MC + k, NDEV, stride=SP), 0:l1 - l0] = a2[8 * v:8 * v + 8, l0:l1]

            def refill():
                fetch(m + NBUF, slot).start()
            if more is None:
                pass
            else:
                pl.when(m + NBUF < MB)(refill)

        @pl.when(c >= 2)
        def _():
            for t in range(1, NDEV):
                send(c - 2, two, t).wait_send()
            own(c - 2, two).wait()

        g = gbuf[...]
        for s in range(NDEV):
            for v in range(IV):
                r0 = s * SP + v * MC
                col = co_ref[pl.ds(pl.multiple_of(c * MC, MC), MC), 8 * v + s:8 * v + s + 1]
                x = jnp.concatenate([abuf[lt, r0:r0 + MC, :] for lt in range(4)], axis=1)
                g = g + x * col
                sbuf[two, s, v] = x.astype(BF16)
        gbuf[...] = g
        for t in range(1, NDEV):
            send(c, two, t).start()
        own(c, two).start()

    @pl.loop(0, NCH - 1)
    def _(c):
        chunk(c, MC, True)
    abuf[...] = jnp.zeros_like(abuf)
    chunk(jnp.int32(NCH - 1), TAIL, None)

    gsend[...] = jnp.broadcast_to(jnp.sum(gbuf[...], axis=0, keepdims=True), (8, QP))

    def gcopy(t):
        return pltpu.make_async_remote_copy(gsend, grecv.at[me], gs_sem.at[t], gr_sem.at[t],
                                            device_id=at(peer(t)), device_id_type=MESH)

    for t in range(1, NDEV):
        gcopy(t).start()
    gown = pltpu.make_async_copy(gsend, grecv.at[me], gs_sem.at[0])
    gown.start()

    for c in (NCH - 2, NCH - 1):
        for t in range(1, NDEV):
            send(c, c % 2, t).wait_send()
        own(c, c % 2).wait()
    for t in range(1, NDEV):
        src = lax.rem(me + NDEV - t, NDEV)
        whole = arecv.at[src // NORB, :, pl.ds(pl.multiple_of(lax.rem(src, NORB) * MP, 8), MP), :]
        pltpu.make_async_remote_copy(whole, whole, rsem.at[t], rsem.at[t],
                                     device_id=at(src), device_id_type=MESH).wait_recv()
        pltpu.make_async_remote_copy(gsend, grecv.at[src], gs_sem.at[t], gr_sem.at[t],
                                     device_id=at(src), device_id_type=MESH).wait()
    gown.wait()
    mcopy.wait()


def half_transform(ints, ct, co, mdiag):
    vmem, hbm = pl.BlockSpec(memory_space=pltpu.VMEM), pl.BlockSpec(memory_space=pl.ANY)
    return pl.pallas_call(
        half_kernel,
        name='half',
        out_shape=(jax.ShapeDtypeStruct((NAUX, IV, NORB * MP, QP), BF16),
                   jax.ShapeDtypeStruct((NDEV, 8, QP), F32),
                   jax.ShapeDtypeStruct((QB, QB), F32)),
        in_specs=[hbm, vmem, vmem, hbm],
        out_specs=(hbm, hbm, hbm),
        scratch_shapes=[
            pltpu.VMEM((NBUF, QB, NB), F32),
            pltpu.VMEM((NSP, 3, QB, NB), BF16),
            pltpu.VMEM((128, NB), BF16),
            pltpu.VMEM((4, NDEV * SP, 128), F32),
            pltpu.VMEM((2, NDEV, IV, MC, QP), BF16),
            pltpu.VMEM((MC, QP), F32),
            pltpu.VMEM((8, QP), F32),
            pltpu.SemaphoreType.DMA((NBUF,)),
            pltpu.SemaphoreType.DMA((2, NDEV)),
            pltpu.SemaphoreType.DMA((NDEV,)),
            pltpu.SemaphoreType.DMA((2,)),
            pltpu.SemaphoreType.DMA((NDEV,)),
            pltpu.SemaphoreType.DMA((NDEV,)),
            pltpu.SemaphoreType.DMA,
            pltpu.SemaphoreType.DMA,
        ],
        compiler_params=pltpu.CompilerParams(collective_id=0, has_side_effects=True, vmem_limit_bytes=60 * 2 ** 20),
    )(ints, ct, co, mdiag)


JBUF = 24


def fock_kernel(b_hbm, a_ref, md_ref, mo_ref, mx_ref, g_ref, k_ref, j_ref,
                ms, ts, jbuf, wb, jp, jsem):
    def fetch(c, slot):
        return pltpu.make_async_copy(b_hbm.at[c], jbuf.at[slot], jsem.at[slot])

    for c in range(JBUF):
        fetch(c, c).start()

    off = mo_ref[...]
    blocks = ((md_ref[...], off), (off.T, mx_ref[...]))

    gam = [jnp.sum(g_ref[r][:, 0:1, 0:QB], axis=0) for r in range(2)]
    fit = [sum(jnp.sum(blocks[r][s] * gam[s], axis=1, keepdims=True) for s in range(2)) for r in range(2)]
    wrow = sum(jnp.sum(blocks[r][0] * fit[r], axis=0, keepdims=True) for r in range(2))
    wb[...] = jnp.broadcast_to(wrow, (128, QB)).T

    ms[...] = jnp.zeros_like(ms)
    for r in range(2):
        for s in range(2):
            parts = split3(blocks[r][s])
            for j in range(3):
                ms[j, r * QP:r * QP + QB, s * QP:s * QP + QB] = parts[j]
    k_ref[...] = jnp.zeros_like(k_ref)

    def coulomb(lo, n):
        @pl.loop(0, n)
        def _(x):
            m = lo + x

            @pl.when(m < MB)
            def _():
                slot = lax.rem(m, JBUF)
                fetch(m, slot).wait()
                acc = [None] * 4
                for g in range(QB // 8):
                    w = wb[8 * g:8 * g + 8, :]
                    for lt in range(4):
                        l0, l1 = lt * 128, min(lt * 128 + 128, NB)
                        y = jbuf[slot, 8 * g:8 * g + 8, l0:l1] * w[:, 0:l1 - l0]
                        acc[lt] = y if acc[lt] is None else acc[lt] + y
                for lt in range(4):
                    l0, l1 = lt * 128, min(lt * 128 + 128, NB)
                    jp[m, :, l0:l1] = acc[lt]

                @pl.when(m + JBUF < MB)
                def _():
                    fetch(m + JBUF, slot).start()

    @pl.loop(0, IV)
    def _(v):
        t = None
        for s in range(2):
            a = a_ref[s, v]
            for j in range(3):
                x = jnp.dot(a, ms[j, s * QP:(s + 1) * QP, :], preferred_element_type=F32)
                t = x if t is None else t + x
        t1, t2, t3 = split3(t)
        ts[0], ts[1], ts[2] = t1, t2, t3
        coulomb(v * 24, 12)
        half = jnp.asarray(0.5, BF16)
        t1, t2, t3 = ts[0], ts[1], ts[2]
        s1 = lax.dot_general(t1, t1 * half, NT, preferred_element_type=F32)
        s1 = s1 + lax.dot_general(t1, t2, NT, preferred_element_type=F32)
        s1 = s1 + lax.dot_general(t1, t3, NT, preferred_element_type=F32)
        s1 = s1 + lax.dot_general(t2, t2 * half, NT, preferred_element_type=F32)
        k_ref[...] += s1
        coulomb(v * 24 + 12, 12)

    j_ref[...] = jnp.sum(jp[...], axis=1)
    k = k_ref[...]
    k_ref[...] = k + k.T


def fock_parts(ints, arecv, md, mo, mx, g):
    vmem, hbm = pl.BlockSpec(memory_space=pltpu.VMEM), pl.BlockSpec(memory_space=pl.ANY)
    return pl.pallas_call(
        fock_kernel,
        name='fock',
        out_shape=(jax.ShapeDtypeStruct((NORB * MP, NORB * MP), F32), jax.ShapeDtypeStruct((MB, NB), F32)),
        in_specs=[hbm] + [vmem] * 5,
        out_specs=(vmem, vmem),
        scratch_shapes=[
            pltpu.VMEM((3, 2 * QP, 2 * QP), BF16),
            pltpu.VMEM((3, NORB * MP, 2 * QP), BF16),
            pltpu.VMEM((JBUF, QB, NB), F32),
            pltpu.VMEM((QB, 128), F32),
            pltpu.VMEM((MB, 8, NB), F32),
            pltpu.SemaphoreType.DMA((JBUF,)),
        ],
        compiler_params=pltpu.CompilerParams(vmem_limit_bytes=63 * 2 ** 20),
    )(ints, arecv, md, mo, mx, g)


def solution(mesh):
    def local_fock(ints, metric, orbitals):
        aux, orb = lax.axis_index('aux'), lax.axis_index('orb')
        c = orbitals[0]
        ints = jnp.transpose(ints, (1, 0, 2))
        co = jnp.pad(lax.dynamic_slice_in_dim(c, orb * MB, MB, 0), ((0, MP - MB), (0, 128 - NI)))
        md = lax.dynamic_slice_in_dim(metric, aux * QB, QB, 1)
        mo = lax.dynamic_slice_in_dim(metric, (1 - aux) * QB, QB, 1)
        arecv, grecv, mx = half_transform(ints, c.T, co, md)
        arecv = jnp.where(aux == 0, arecv, arecv[::-1])
        g = grecv.reshape(NAUX, NORB, 8, QP)
        g = jnp.where(aux == 0, g, g[::-1])
        k, j = fock_parts(ints, arecv, md, mo, mx, g)
        k = k.reshape(NORB, MP, NORB, MP)[:, :MB, :, :MB].reshape(NB, NB)
        krow = lax.psum_scatter(k, 'orb', scatter_dimension=0, tiled=True)
        fock = 2.0 * j - krow
        return lax.psum_scatter(fock, 'aux', scatter_dimension=1, tiled=True)[None]

    return jax.shard_map(local_fock, mesh=mesh,
                         in_specs=(P(('sys', 'aux'), 'orb', None), P(('sys', 'aux'), None), P('sys', None, None)),
                         out_specs=P('sys', 'orb', 'aux'), check_vma=False)
```

time: 721 us -> 230 us (0.32); the launches traced: 708 us -> 229 us
  waiting for transfers between devices: 359 us -> 19.6 us
  matrix products: 272 us -> 0 us
  Pallas kernels: 0 us -> 151 us
  local copies, waits for them, and re-layouts: 35 us -> 10.7 us
  other arithmetic: 0 us -> 8.96 us
    all_gather x2 -> x0, waiting for transfers between devices: 351 us -> none  [the longest x1 180 us: local_fock(): half_all = lax.all_gather(half_tr, 'aux', axis=0, tiled=True)]
    dot_general x6 -> x0, matrix products: 268 us -> none  [the longest x1 102 us: local_fock(): jnp.einsum('qml,dli->qmdi', ints_blk, orbitals, precision=PRECISE, prefer...]
    pallas_call x0 -> x2, Pallas kernels: none -> 151 us  [the longest x1 99.5 us: half_transform(): pl.pallas_call(half_kernel, name='half', out_shape=(jax.ShapeDtypeStruct(...]
    unnamed x0 -> x1, blocking collectives: none -> 22.8 us
    all_gather x1 -> x0, local copies, waits for them, and re-layouts: 19.7 us -> none  [local_fock(): half_all = lax.all_gather(half_tr, 'aux', axis=0, tiled=True)]
    another operation x1 -> x0, blocking collectives: 18.1 us -> none
    dot_general x2 -> x0, local copies, waits for them, and re-layouts: 11.9 us -> none  [the longest x1 11.8 us: local_fock(): jnp.einsum('qml,dli->qmdi', ints_blk, orbitals, precision=PRECISE, prefer...]
    unnamed x6 -> x3, waiting for transfers between devices: 8.85 us -> 19.6 us
  transfers between devices with their start and end apart: 4 -> 2, of which waited for: 3 -> 1; matrix products, arithmetic and copies ran while one was open for 18% -> 1% of each run, Pallas kernels for 0% -> 0%
where the time goes in v1:
time: 230 us; the launch traced here: 229 us
  Pallas kernels  151 us (66%)
  blocking collectives  22.8 us (10%)
  waiting for transfers between devices  19.6 us (9%)
  between operations  14.8 us (6%)
  local copies, waits for them, and re-layouts  10.7 us (5%)
  other arithmetic  8.96 us (4%)
    pallas_call x1, Pallas kernels, half_transform(): pl.pallas_call(half_kernel, name='half', out_shape=(jax.ShapeDtypeStruct(...  99.5 us
    pallas_call x1, Pallas kernels, fock_parts(): pl.pallas_call(fock_kernel, name='fock', out_shape=(jax.ShapeDtypeStruct(...  51.6 us
    unnamed x1, blocking collectives  22.8 us
    unnamed x3, waiting for transfers between devices  19.6 us
    select_n x1, other arithmetic, local_fock(): arecv = jnp.where(aux == 0, arecv, arecv[::-1])  7.56 us
  transfers between devices with their start and end apart: 2, of which 1 were waited for; matrix products, arithmetic and copies ran while one was open for 1% of the time, Pallas kernels for 0%

profile of v1, /device:TPU:0, one launch (start us, length us, event | category | flops | bytes accessed | tf_op | source)
XLA Modules:
  0.0 229.4 jit_solution(7013395732273506164)
XLA Ops:
  6.5 0.0 all-reduce.6.cloned.1.call-start
  6.5 0.9 constant_dynamic-slice_fusion.2
  7.4 0.1 copy.6
  7.5 0.6 pad.4.co_ref
  8.1 3.5 %constant_dynamic-slice_fusion = (f32[464,464]{1,0:T(8,128)}, f32[464,464]{1,0:T(8,128)}) fusion(f32[464,928]{1,0:T(8,128)} %param.4, s32[]{:T(128)S(6)} %select_n.29, s32[]{:T(128)S(6)} %select_n.27), kind=kLoop, calls=%fused_computation.4 | loop fusion | bytes 3444744 | tf_op jit(solution)/shard_map/dynamic_slice | solution.py:287
  11.6 99.5 %half.1 = (bf16[2,5,480,512]{3,2,1,0:T(8,128)(2,1)}, f32[8,8,512]{2,1,0:T(8,128)}, f32[464,464]{1,0:T(8,128)}) custom-call(f32[116,464,464]{2,1,0:T(8,128)} %bitcast.2.b_hbm, f32[40,464]{1,0:T(8,128)} %bitcast.16, f32[120,128]{1,0:T(8,128)} %pad.4.co_ref, f32[464,464]{1,0:T(8,128)} %get-tuple-element.16.md_hbm.md_ref), custom_call_target="tpu_custom_call" | custom-call | tf_op jit(solution)/shard_map/half/pallas_call | solution.py:155
  111.1 0.0 copy-start.1
  111.1 7.6 %reverse_select_fusion.a_ref = bf16[2,5,480,512]{3,2,1,0:T(8,128)(2,1)} fusion(bf16[2,5,480,512]{3,2,1,0:T(8,128)(2,1)} %get-tuple-element.10, pred[]{:T(512)S(6)} %eq.4), kind=kLoop, calls=%fused_computation | loop fusion | flops 2457600 | bytes 9830401 | tf_op jit(solution)/shard_map/jit(_where)/select_n | solution.py:289
  118.7 0.0 copy-done.1
  118.7 0.7 reverse_select_fusion.1.g_ref
  119.3 51.6 %fock.1 = (f32[480,480]{1,0:T(8,128)}, f32[116,464]{1,0:T(8,128)}) custom-call(f32[116,464,464]{2,1,0:T(8,128)} %bitcast.2.b_hbm, bf16[2,5,480,512]{3,2,1,0:T(8,128)(2,1)} %reverse_select_fusion.a_ref, f32[464,464]{1,0:T(8,128)} %get-tuple-element.16.md_hbm.md_ref, f32[464,464]{1,0:T(8,128)} %get-tuple-element.15.mo_ref, ...), custom_call_target="tpu_custom_call" | custom-call | tf_op jit(solution)/shard_map/fock/pallas_call | solution.py:262
  171.0 0.0 copy-start.2
  171.0 0.0 copy-start
  171.0 0.0 copy-start.3
  171.0 1.9 reshape.11
  172.9 0.1 slice.4
  172.9 0.4 reshape.12
  173.4 22.8 %fusion = f32[128,464]{1,0:T(8,128)S(1)} fusion(f32[464,464]{1,0:T(8,128)S(1)} %reshape.12), kind=kCustom, calls=%all-reduce-scatter | all-reduce-scatter fusion | flops 237569 | bytes 1099264
  196.2 1.3 collective-permute-start
  197.5 0.0 copy-done.2
  197.5 0.6 dynamic-slice.7
  198.7 0.0 collective-permute-done
  198.7 0.3 concatenate
  199.1 0.0 copy-done
  199.1 0.7 dynamic-slice_subtract_fusion
  199.8 0.0 all-reduce.6.cloned.1.call-update
  199.8 0.0 copy-done.3
  199.9 0.6 dynamic-slice.3
  201.1 19.6 %all-reduce.6.cloned.1.call-done = f32[116,464]{1,0:T(8,128)} async-done(((f32[116,464]{1,0:T(8,128)}), f32[116,464]{1,0:T(8,128)}) %all-reduce.6.cloned.1.call-update) | async-done | bytes 215312
  220.7 1.0 dynamic-slice_bitcast_fusion
  221.7 0.8 copy.7
  (1 shorter events, 0.0 us)
Async XLA Ops:
  6.5 214.2 %all-reduce.6.cloned.1.call-start = ((), (), s32[]{:S(2)}) async-start(), calls=%async_computation | async-start | bytes 491520
  111.1 7.6 %copy-start.1 = (f32[8,8,512]{2,1,0:T(8,128)S(1)}, f32[8,8,512]{2,1,0:T(8,128)}, u32[]{:S(2)}) copy-start(f32[8,8,512]{2,1,0:T(8,128)} %get-tuple-element.12) | copy-start | bytes 393220
  171.0 26.5 %copy-start.2 = (u32[8]{0:T(128)S(1)}, u32[8]{0:T(128)}, u32[]{:S(2)}) copy-start(u32[8]{0:T(128)} %constant.28) | copy-start | bytes 100
  171.0 28.1 %copy-start = (f32[116,464]{1,0:T(8,128)S(1)}, f32[116,464]{1,0:T(8,128)}, u32[]{:S(2)}) copy-start(f32[116,464]{1,0:T(8,128)} %get-tuple-element.13) | copy-start | bytes 645892
  171.0 28.9 %copy-start.3 = (u32[8]{0:T(128)S(1)}, u32[8]{0:T(128)}, u32[]{:S(2)}) copy-start(u32[8]{0:T(128)} %constant.32) | copy-start | bytes 100
  196.2 2.6 %collective-permute-start = (f32[36,464]{1,0:T(8,128)S(1)}, f32[36,464]{1,0:T(8,128)S(1)}, u32[]{:S(2)}, u32[]{:S(2)}) collective-permute-start(f32[36,464]{1,0:T(8,128)S(1)} %slice.5), channel_id=1, source_target_pairs={{0,1},{1,2},{2,3},{4,5},{5,6},{6,7}} | collective-permute-start | bytes 200456
Sparse Core Ops, SparseCore 0:
  200.0 20.7 all-reduce.5

commit v2 on v1

--- a/solution.py
+++ b/solution.py
@@ -17,8 +17,9 @@
 NCH = MP // MC
 TAIL = MB - MC * (NCH - 1)
 SP = 48
-NBUF = 12
-NSP = 4
+GR = 4
+NG = MB // GR
+NBUF = 4
 
 
 def split3(x):
@@ -41,11 +42,12 @@
     def peer(t):
         return lax.rem(me + t, NDEV)
 
-    def fetch(m, slot):
-        return pltpu.make_async_copy(b_hbm.at[m], bbuf.at[slot], bsem.at[slot])
-
-    for m in range(NBUF):
-        fetch(m, m).start()
+    def fetch(g):
+        slot = g % NBUF if isinstance(g, int) else lax.rem(g, NBUF)
+        return pltpu.make_async_copy(b_hbm.at[pl.ds(g * GR, GR)], bbuf.at[slot], bsem.at[slot])
+
+    for g in range(NBUF - 1):
+        fetch(g).start()
 
     barrier = pltpu.get_barrier_semaphore()
     for t in range(1, NDEV):
@@ -73,18 +75,19 @@
     def own(c, slot):
         return pltpu.make_async_copy(sbuf.at[slot, me], place(c), osem.at[slot])
 
-    def chunk(c, rows, more):
-        two = lax.rem(c, 2)
-        for k in range(rows):
-            m = c * MC + k
-            slot = lax.rem(m, NBUF)
-            fetch(m, slot).wait()
-            parts = split3(bbuf[slot])
+    def cut(g, half):
+        slot = lax.rem(g, NBUF)
+        for k in range(GR):
+            for r in range(0, QB, 16):
+                parts = split3(bbuf[slot, k, r:r + 16, :])
+                for j in range(3):
+                    bs[half * GR + k, j, r:r + 16, :] = parts[j]
+
+    def dots(half):
+        for k in range(half * GR, (half + 1) * GR):
             r = None
             for j in range(3):
-                bs[k % NSP, j] = parts[j]
-            for j in range(3):
-                x = lax.dot_general(cw[...], bs[k % NSP, j], NT, preferred_element_type=F32)
+                x = lax.dot_general(cw[...], bs[k, j], NT, preferred_element_type=F32)
                 r = x if r is None else r + x
             a2 = r[0:NI] + r[NI:2 * NI] + r[2 * NI:3 * NI]
             for v in range(IV):
@@ -92,19 +95,8 @@
                     l0, l1 = lt * 128, min(lt * 128 + 128, QB)
                     abuf[lt, pl.ds(v * MC + k, NDEV, stride=SP), 0:l1 - l0] = a2[8 * v:8 * v + 8, l0:l1]
 
-            def refill():
-                fetch(m + NBUF, slot).start()
-            if more is None:
-                pass
-            else:
-                pl.when(m + NBUF < MB)(refill)
-
-        @pl.when(c >= 2)
-        def _():
-            for t in range(1, NDEV):
-                send(c - 2, two, t).wait_send()
-            own(c - 2, two).wait()
-
+    def deliver(c):
+        two = lax.rem(c, 2)
         g = gbuf[...]
         for s in range(NDEV):
             for v in range(IV):
@@ -118,11 +110,42 @@
             send(c, two, t).start()
         own(c, two).start()
 
+    def reuse(c):
+        two = lax.rem(c, 2)
+
+        @pl.when(c >= 2)
+        def _():
+            for t in range(1, NDEV):
+                send(c - 2, two, t).wait_send()
+            own(c - 2, two).wait()
+
+    fetch(0).wait()
+    cut(jnp.int32(0), 0)
+
     @pl.loop(0, NCH - 1)
     def _(c):
-        chunk(c, MC, True)
+        fetch(2 * c + 1).wait()
+        fetch(2 * c + 2).wait()
+
+        @pl.when(2 * c + 3 < NG)
+        def _():
+            fetch(2 * c + 3).start()
+
+        @pl.when(2 * c + 4 < NG)
+        def _():
+            fetch(2 * c + 4).start()
+
+        reuse(c)
+        cut(2 * c + 1, 1)
+        dots(0)
+        cut(2 * c + 2, 0)
+        dots(1)
+        deliver(c)
+
+    reuse(jnp.int32(NCH - 1))
     abuf[...] = jnp.zeros_like(abuf)
-    chunk(jnp.int32(NCH - 1), TAIL, None)
+    dots(0)
+    deliver(jnp.int32(NCH - 1))
 
     gsend[...] = jnp.broadcast_to(jnp.sum(gbuf[...], axis=0, keepdims=True), (8, QP))
 
@@ -161,8 +184,8 @@
         in_specs=[hbm, vmem, vmem, hbm],
         out_specs=(hbm, hbm, hbm),
         scratch_shapes=[
-            pltpu.VMEM((NBUF, QB, NB), F32),
-            pltpu.VMEM((NSP, 3, QB, NB), BF16),
+            pltpu.VMEM((NBUF, GR, QB, NB), F32),
+            pltpu.VMEM((2 * GR, 3, QB, NB), BF16),
             pltpu.VMEM((128, NB), BF16),
             pltpu.VMEM((4, NDEV * SP, 128), F32),
             pltpu.VMEM((2, NDEV, IV, MC, QP), BF16),
@@ -181,21 +204,33 @@
     )(ints, ct, co, mdiag)
 
 
-JBUF = 24
-
-
-def fock_kernel(b_hbm, a_ref, md_ref, mo_ref, mx_ref, g_ref, k_ref, j_ref,
-                ms, ts, jbuf, wb, jp, jsem):
-    def fetch(c, slot):
-        return pltpu.make_async_copy(b_hbm.at[c], jbuf.at[slot], jsem.at[slot])
-
-    for c in range(JBUF):
+JB = 12
+OB = NB // NAUX
+
+
+def fock_kernel(b_hbm, a_ref, md_ref, mo_ref, mx_ref, g_ref, out_ref,
+                ms, ts, jbuf, wb, jp, kacc, kout, kin, jsem, ssem, rsem):
+    aux, orb = lax.axis_index('aux'), lax.axis_index('orb')
+    me = aux * NORB + orb
+    side = (aux, 1 - aux)
+
+    def at(d):
+        return {'aux': d // NORB, 'orb': lax.rem(d, NORB)}
+
+    def fetch(m, slot):
+        return pltpu.make_async_copy(b_hbm.at[m], jbuf.at[slot], jsem.at[slot])
+
+    for c in range(2 * JB):
         fetch(c, c).start()
+
+    barrier = pltpu.get_barrier_semaphore()
+    for t in range(1, NDEV):
+        pl.semaphore_signal(barrier, inc=1, device_id=at(lax.rem(me + t, NDEV)), device_id_type=MESH)
 
     off = mo_ref[...]
     blocks = ((md_ref[...], off), (off.T, mx_ref[...]))
 
-    gam = [jnp.sum(g_ref[r][:, 0:1, 0:QB], axis=0) for r in range(2)]
+    gam = [sum(g_ref[side[r] * NORB + o][0:1, 0:QB] for o in range(NORB)) for r in range(2)]
     fit = [sum(jnp.sum(blocks[r][s] * gam[s], axis=1, keepdims=True) for s in range(2)) for r in range(2)]
     wrow = sum(jnp.sum(blocks[r][0] * fit[r], axis=0, keepdims=True) for r in range(2))
     wb[...] = jnp.broadcast_to(wrow, (128, QB)).T
@@ -206,55 +241,82 @@
             parts = split3(blocks[r][s])
             for j in range(3):
                 ms[j, r * QP:r * QP + QB, s * QP:s * QP + QB] = parts[j]
-    k_ref[...] = jnp.zeros_like(k_ref)
-
-    def coulomb(lo, n):
-        @pl.loop(0, n)
-        def _(x):
-            m = lo + x
-
-            @pl.when(m < MB)
+    kacc[...] = jnp.zeros_like(kacc)
+
+    def arrive(lo, base):
+        for x in range(JB):
+            @pl.when(lo + x < MB)
             def _():
-                slot = lax.rem(m, JBUF)
-                fetch(m, slot).wait()
-                acc = [None] * 4
-                for g in range(QB // 8):
-                    w = wb[8 * g:8 * g + 8, :]
-                    for lt in range(4):
-                        l0, l1 = lt * 128, min(lt * 128 + 128, NB)
-                        y = jbuf[slot, 8 * g:8 * g + 8, l0:l1] * w[:, 0:l1 - l0]
-                        acc[lt] = y if acc[lt] is None else acc[lt] + y
+                fetch(lo + x, base + x).wait()
+
+    def coulomb(lo, base):
+        for x in range(JB):
+            acc = [None] * 4
+            for g in range(QB // 8):
+                w = wb[8 * g:8 * g + 8, :]
                 for lt in range(4):
                     l0, l1 = lt * 128, min(lt * 128 + 128, NB)
-                    jp[m, :, l0:l1] = acc[lt]
-
-                @pl.when(m + JBUF < MB)
-                def _():
-                    fetch(m + JBUF, slot).start()
+                    y = jbuf[base + x, 8 * g:8 * g + 8, l0:l1] * w[:, 0:l1 - l0]
+                    acc[lt] = y if acc[lt] is None else acc[lt] + y
+            for lt in range(4):
+                l0, l1 = lt * 128, min(lt * 128 + 128, NB)
+                jp[lo + x, :, l0:l1] = acc[lt]
+
+    def refill(lo, base):
+        for x in range(JB):
+            @pl.when(lo + 2 * JB + x < MB)
+            def _():
+                fetch(lo + 2 * JB + x, base + x).start()
 
     @pl.loop(0, IV)
     def _(v):
+        lo = v * 2 * JB
+        arrive(lo, 0)
         t = None
         for s in range(2):
-            a = a_ref[s, v]
+            a = a_ref[side[s], v]
             for j in range(3):
                 x = jnp.dot(a, ms[j, s * QP:(s + 1) * QP, :], preferred_element_type=F32)
                 t = x if t is None else t + x
-        t1, t2, t3 = split3(t)
-        ts[0], ts[1], ts[2] = t1, t2, t3
-        coulomb(v * 24, 12)
+        ts[0], ts[1], ts[2] = split3(t)
+        coulomb(lo, 0)
+        refill(lo, 0)
+        arrive(lo + JB, JB)
         half = jnp.asarray(0.5, BF16)
         t1, t2, t3 = ts[0], ts[1], ts[2]
         s1 = lax.dot_general(t1, t1 * half, NT, preferred_element_type=F32)
         s1 = s1 + lax.dot_general(t1, t2, NT, preferred_element_type=F32)
         s1 = s1 + lax.dot_general(t1, t3, NT, preferred_element_type=F32)
         s1 = s1 + lax.dot_general(t2, t2 * half, NT, preferred_element_type=F32)
-        k_ref[...] += s1
-        coulomb(v * 24 + 12, 12)
-
-    j_ref[...] = jnp.sum(jp[...], axis=1)
-    k = k_ref[...]
-    k_ref[...] = k + k.T
+        kacc[...] += s1
+        coulomb(lo + JB, JB)
+        refill(lo + JB, JB)
+
+    k = kacc[...]
+    k = k + k.T
+    for a in range(NAUX):
+        cols = jnp.concatenate([k[:, o * MP:o * MP + MB] for o in (2 * a, 2 * a + 1)], axis=1)
+        for o in range(NORB):
+            kout[a * NORB + o, :, 0:OB] = -cols[o * MP:(o + 1) * MP]
+    j = jnp.sum(jp[...], axis=1)
+    for a in range(NAUX):
+        kout[a * NORB + orb, :, 0:OB] += 2.0 * j[:, a * OB:(a + 1) * OB]
+
+    def send(t):
+        d = lax.rem(me + t, NDEV)
+        return pltpu.make_async_remote_copy(kout.at[d], kin.at[t], ssem.at[t], rsem.at[t],
+                                            device_id=at(d), device_id_type=MESH)
+
+    pl.semaphore_wait(barrier, NDEV - 1)
+    for t in range(1, NDEV):
+        send(t).start()
+    total = kout[me]
+    for t in range(1, NDEV):
+        send(t).wait_recv()
+        total = total + kin[t]
+    out_ref[...] = total[0:MB, 0:OB]
+    for t in range(1, NDEV):
+        send(t).wait_send()
 
 
 def fock_parts(ints, arecv, md, mo, mx, g):
@@ -262,18 +324,23 @@
     return pl.pallas_call(
         fock_kernel,
         name='fock',
-        out_shape=(jax.ShapeDtypeStruct((NORB * MP, NORB * MP), F32), jax.ShapeDtypeStruct((MB, NB), F32)),
+        out_shape=jax.ShapeDtypeStruct((MB, OB), F32),
         in_specs=[hbm] + [vmem] * 5,
-        out_specs=(vmem, vmem),
+        out_specs=vmem,
         scratch_shapes=[
             pltpu.VMEM((3, 2 * QP, 2 * QP), BF16),
             pltpu.VMEM((3, NORB * MP, 2 * QP), BF16),
-            pltpu.VMEM((JBUF, QB, NB), F32),
+            pltpu.VMEM((2 * JB, QB, NB), F32),
             pltpu.VMEM((QB, 128), F32),
-            pltpu.VMEM((MB, 8, NB), F32),
-            pltpu.SemaphoreType.DMA((JBUF,)),
+            pltpu.VMEM((MP, 8, NB), F32),
+            pltpu.VMEM((NORB * MP, NORB * MP), F32),
+            pltpu.VMEM((NDEV, MP, 256), F32),
+            pltpu.VMEM((NDEV, MP, 256), F32),
+            pltpu.SemaphoreType.DMA((2 * JB,)),
+            pltpu.SemaphoreType.DMA((NDEV,)),
+            pltpu.SemaphoreType.DMA((NDEV,)),
         ],
-        compiler_params=pltpu.CompilerParams(vmem_limit_bytes=63 * 2 ** 20),
+        compiler_params=pltpu.CompilerParams(collective_id=1, has_side_effects=True, vmem_limit_bytes=63 * 2 ** 20),
     )(ints, arecv, md, mo, mx, g)
 
 
@@ -286,14 +353,7 @@
         md = lax.dynamic_slice_in_dim(metric, aux * QB, QB, 1)
         mo = lax.dynamic_slice_in_dim(metric, (1 - aux) * QB, QB, 1)
         arecv, grecv, mx = half_transform(ints, c.T, co, md)
-        arecv = jnp.where(aux == 0, arecv, arecv[::-1])
-        g = grecv.reshape(NAUX, NORB, 8, QP)
-        g = jnp.where(aux == 0, g, g[::-1])
-        k, j = fock_parts(ints, arecv, md, mo, mx, g)
-        k = k.reshape(NORB, MP, NORB, MP)[:, :MB, :, :MB].reshape(NB, NB)
-        krow = lax.psum_scatter(k, 'orb', scatter_dimension=0, tiled=True)
-        fock = 2.0 * j - krow
-        return lax.psum_scatter(fock, 'aux', scatter_dimension=1, tiled=True)[None]
+        return fock_parts(ints, arecv, md, mo, mx, grecv)[None]
 
     return jax.shard_map(local_fock, mesh=mesh,
                          in_specs=(P(('sys', 'aux'), 'orb', None), P(('sys', 'aux'), None), P('sys', None, None)),

time: 230 us -> 159 us (0.69)
  blocking collectives: 22.8 us -> 0 us
  waiting for transfers between devices: 19.6 us -> 0 us
  between operations: 14.8 us -> 0.02 us
  other arithmetic: 8.96 us -> 0 us
  local copies, waits for them, and re-layouts: 10.7 us -> 6.74 us
    unnamed x1 -> x0, blocking collectives: 22.8 us -> none
    unnamed x3 -> x0, waiting for transfers between devices: 19.6 us -> none
    pallas_call x1, Pallas kernels: 51.6 us -> 61.4 us  [fock_parts(): pl.pallas_call(fock_kernel, name='fock', out_shape=jax.ShapeDtypeStruct((...]
    pallas_call x1, Pallas kernels: 99.5 us -> 89.7 us  [half_transform(): pl.pallas_call(half_kernel, name='half', out_shape=(jax.ShapeDtypeStruct(...]
    select_n x2 -> x0, other arithmetic: 8.23 us -> none  [the longest x1 7.56 us: local_fock(): arecv = jnp.where(aux == 0, arecv, arecv[::-1])]
  transfers between devices with their start and end apart: 2 -> 0, of which waited for: 1 -> 0; matrix products, arithmetic and copies ran while one was open for 1% -> 0% of each run, Pallas kernels for 0% -> 0%
where the time goes in v2:
time: 159 us; the launch traced here: 158 us
  Pallas kernels  151 us (95%)
  local copies, waits for them, and re-layouts  6.74 us (4%)
    pallas_call x1, Pallas kernels, half_transform(): pl.pallas_call(half_kernel, name='half', out_shape=(jax.ShapeDtypeStruct(...  89.7 us
    pallas_call x1, Pallas kernels, fock_parts(): pl.pallas_call(fock_kernel, name='fock', out_shape=jax.ShapeDtypeStruct((...  61.4 us
    dynamic_slice x1, local copies, waits for them, and re-layouts, local_fock(): mo = lax.dynamic_slice_in_dim(metric, (1 - aux) * QB, QB, 1)  3.47 us

profile of v2, /device:TPU:0, one launch (start us, length us, event | category | flops | bytes accessed | tf_op | source)
XLA Modules:
  0.0 157.9 jit_solution(9518566863235620592)
XLA Ops:
  0.0 0.9 constant_dynamic-slice_fusion.2
  0.9 0.1 copy.4
  1.0 0.6 pad.4.co_ref
  1.6 3.5 %constant_dynamic-slice_fusion = (f32[464,464]{1,0:T(8,128)}, f32[464,464]{1,0:T(8,128)}) fusion(f32[464,928]{1,0:T(8,128)} %param.4, s32[]{:T(128)S(6)} %select_n.11, s32[]{:T(128)S(6)} %select_n.10), kind=kLoop, calls=%fused_computation | loop fusion | bytes 3444744 | tf_op jit(solution)/shard_map/dynamic_slice | solution.py:354
  5.1 89.7 %half.1 = (bf16[2,5,480,512]{3,2,1,0:T(8,128)(2,1)}, f32[8,8,512]{2,1,0:T(8,128)}, f32[464,464]{1,0:T(8,128)}) custom-call(f32[116,464,464]{2,1,0:T(8,128)} %bitcast.b_hbm, f32[40,464]{1,0:T(8,128)} %bitcast.8, f32[120,128]{1,0:T(8,128)} %pad.4.co_ref, f32[464,464]{1,0:T(8,128)} %get-tuple-element.12.md_hbm.md_ref), custom_call_target="tpu_custom_call" | custom-call | tf_op jit(solution)/shard_map/half/pallas_call | solution.py:178
  94.8 61.4 %fock.1 = f32[116,232]{1,0:T(8,128)} custom-call(f32[116,464,464]{2,1,0:T(8,128)} %bitcast.b_hbm, bf16[2,5,480,512]{3,2,1,0:T(8,128)(2,1)} %get-tuple-element.8.a_ref, f32[464,464]{1,0:T(8,128)} %get-tuple-element.12.md_hbm.md_ref, f32[464,464]{1,0:T(8,128)} %get-tuple-element.11.mo_ref, f32[464,464]{1,0:T(8,128)} %get-tuple-element.9.mx_ref, ...), custom_call_target="tpu_custom_call" | custom-call | tf_op jit(solution)/shard_map/fock/pallas_call | solution.py:324
  156.3 1.7 %copy.5 = f32[1,116,232]{2,0,1:T(1,128)} copy(f32[1,116,232]{2,1,0:T(8,128)} %bitcast.6) | data formatting | bytes 215296 | tf_op jit(solution)/shard_map/broadcast_in_dim | solution.py:356

commit v3 on v2

v3 whole, which is shorter than its diff:
```python
import jax
import jax.numpy as jnp
from jax import lax
from jax.experimental import pallas as pl
from jax.experimental.pallas import tpu as pltpu

P = jax.sharding.PartitionSpec
F32, BF16 = jnp.float32, jnp.bfloat16
MESH = pl.DeviceIdType.MESH
NT = (((1,), (1,)), ((), ()))
LN2 = 0.6931471805599453
TOP = 126.0
ROUND = 1.5 * 2.0 ** 15

NAUX, NORB, NDEV = 2, 4, 8
QB, MB, NB, NI = 464, 116, 464, 40
IV = NI // NDEV
QP, MP = 512, 120
MC = 8
NCH = MP // MC
TAIL = MB - MC * (NCH - 1)
SP = 48
GR = 4
NG = MB // GR
NBUF = 4
NST = (NG + 1) // 2
OB = NB // NAUX
HQ = QB // 2


def split3(x):
    a = x.astype(BF16)
    r = x - a.astype(F32)
    b = r.astype(BF16)
    c = (r - b.astype(F32)).astype(BF16)
    return a, b, c


def kernel(b_hbm, ct_ref, co_ref, m_ref, out_ref,
           bbuf, bs, cw, abuf, sbuf, arecv, own, gbuf, gsend, grecv,
           md, mx, ms, aspl, af, ts, wb, jp, kacc, kout, kin,
           bsem, ssem, rsem, gs_sem, gr_sem, ms_sem, mr_sem, ks_sem, kr_sem):
    aux, orb = lax.axis_index('aux'), lax.axis_index('orb')
    me = aux * NORB + orb
    core = lax.rem(orb, 2)
    side = (aux, 1 - aux)

    def at(d):
        return {'aux': d // NORB, 'orb': lax.rem(d, NORB)}

    def peer(t):
        return lax.rem(me + t, NDEV)

    def fetch(g):
        slot = g % NBUF if isinstance(g, int) else lax.rem(g, NBUF)
        return pltpu.make_async_copy(b_hbm.at[pl.ds(g * GR, GR)], bbuf.at[slot], bsem.at[slot])

    for g in range(NBUF - 1):
        fetch(g).start()

    barrier = pltpu.get_barrier_semaphore()
    for t in range(1, NDEV):
        pl.semaphore_signal(barrier, inc=1, device_id=at(peer(t)), device_id_type=MESH)

    for a in range(NAUX):
        @pl.when(aux == a)
        def _():
            md[...] = m_ref[:, a * QB:(a + 1) * QB]

    abuf[...] = jnp.zeros_like(abuf)
    gbuf[...] = jnp.zeros_like(gbuf)
    c1, c2, c3 = split3(ct_ref[...])
    cw[...] = jnp.concatenate(
        [c1.astype(F32), c2.astype(F32), c3.astype(F32), jnp.zeros((8, NB), F32)], axis=0).astype(BF16)

    pl.semaphore_wait(barrier, NDEV - 1)

    def mcopy(src, k, rows, dev):
        block = pl.ds(pl.multiple_of(rows * HQ, 8), HQ)
        return pltpu.make_async_remote_copy(src.at[block], mx.at[block], ms_sem.at[k], mr_sem.at[k],
                                            device_id=dev, device_id_type=MESH)
    mfirst = mcopy(md, 0, core, {'aux': 1 - aux, 'orb': orb})
    mfirst.start()

    def send(c, slot, t):
        d = peer(t)
        return pltpu.make_async_remote_copy(sbuf.at[slot, d], arecv.at[aux, :, orb * NCH + c],
                                            ssem.at[slot, t], rsem.at[t], device_id=at(d), device_id_type=MESH)

    def cut(g, half):
        slot = lax.rem(g, NBUF)
        for k in range(GR):
            for r in range(0, QB, 16):
                parts = split3(bbuf[slot, k, r:r + 16, :])
                for j in range(3):
                    bs[half * GR + k, j, r:r + 16, :] = parts[j]

    def dots(half):
        for k in range(half * GR, (half + 1) * GR):
            r = None
            for j in range(3):
                x = lax.dot_general(cw[...], bs[k, j], NT, preferred_element_type=F32)
                r = x if r is None else r + x
            a2 = r[0:NI] + r[NI:2 * NI] + r[2 * NI:3 * NI]
            for v in range(IV):
                for lt in range(4):
                    l0, l1 = lt * 128, min(lt * 128 + 128, QB)
                    abuf[lt, pl.ds(v * MC + k, NDEV, stride=SP), 0:l1 - l0] = a2[8 * v:8 * v + 8, l0:l1]

    lane = lax.broadcasted_iota(jnp.int32, (MC, QP), 1)

    def deliver(c):
        two = lax.rem(c, 2)
        g = gbuf[...]
        for s in range(NDEV):
            for v in range(IV):
                r0 = s * SP + v * MC
                col = co_ref[pl.ds(pl.multiple_of(c * MC, MC), MC), 8 * v + s:8 * v + s + 1]
                x = jnp.concatenate([abuf[lt, r0:r0 + MC, :] for lt in range(4)], axis=1)
                g = g + x * col
                big = jnp.maximum(jnp.max(jnp.abs(x), axis=1, keepdims=True), 2.0 ** -100)
                j = jnp.ceil(jnp.log(big * (1.0 / TOP)) * (1.0 / LN2) + 0.01)
                up = jnp.exp2(j).astype(BF16).astype(F32)
                down = jnp.exp2(-j).astype(BF16).astype(F32)
                y = jnp.exp2(x * down)
                sbuf[two, s, v] = jnp.where(lane < QB, y, up).astype(BF16)
        gbuf[...] = g
        for v in range(IV):
            r0 = pl.multiple_of(me * SP + v * MC, 8)
            own[v, pl.ds(pl.multiple_of(c * MC, MC), MC), :] = jnp.concatenate(
                [abuf[lt, pl.ds(r0, MC), :] for lt in range(4)], axis=1)
        for t in range(1, NDEV):
            send(c, two, t).start()

    def reuse(c):
        two = lax.rem(c, 2)

        @pl.when(c >= 2)
        def _():
            for t in range(1, NDEV):
                send(c - 2, two, t).wait_send()

    fetch(0).wait()
    cut(jnp.int32(0), 0)

    @pl.loop(0, NCH - 1)
    def _(c):
        fetch(2 * c + 1).wait()
        fetch(2 * c + 2).wait()

        @pl.when(2 * c + 3 < NG)
        def _():
            fetch(2 * c + 3).start()

        @pl.when(2 * c + 4 < NG)
        def _():
            fetch(2 * c + 4).start()

        reuse(c)
        cut(2 * c + 1, 1)
        dots(0)
        cut(2 * c + 2, 0)
        dots(1)
        deliver(c)

    for g in range(NBUF):
        fetch(g).start()
    reuse(jnp.int32(NCH - 1))
    abuf[...] = jnp.zeros_like(abuf)
    dots(0)
    deliver(jnp.int32(NCH - 1))

    gsend[...] = jnp.broadcast_to(jnp.sum(gbuf[...], axis=0, keepdims=True), (8, QP))

    def gcopy(t):
        return pltpu.make_async_remote_copy(gsend, grecv.at[me], gs_sem.at[t], gr_sem.at[t],
                                            device_id=at(peer(t)), device_id_type=MESH)

    for t in range(1, NDEV):
        gcopy(t).start()
    grecv[me] = gsend[...]

    mfirst.wait()
    msecond = mcopy(mx, 1, core, {'orb': orb + 1 - 2 * core})
    msecond.start()

    ms[...] = jnp.zeros_like(ms)

    def parts_of(x, r, s):
        parts = split3(x)
        for j in range(3):
            ms[j, r * QP:r * QP + QB, s * QP:s * QP + QB] = parts[j]

    parts_of(md[...], 0, 0)
    for a in range(NAUX):
        @pl.when(aux == a)
        def _():
            off = m_ref[:, (1 - a) * QB:(2 - a) * QB]
            af[0:QB, 0:QB] = off
    parts_of(af[0:QB, 0:QB], 0, 1)
    parts_of(af[0:QB, 0:QB].T, 1, 0)
    msecond.wait_send()
    mcopy(mx, 1, 1 - core, {'orb': orb + 1 - 2 * core}).wait_recv()
    parts_of(mx[...], 1, 1)
    kacc[...] = jnp.zeros_like(kacc)

    for t in range(1, NDEV):
        src = lax.rem(me + NDEV - t, NDEV)
        pltpu.make_async_remote_copy(gsend, grecv.at[src], gs_sem.at[t], gr_sem.at[t],
                                     device_id=at(src), device_id_type=MESH).wait()
    off = af[0:QB, 0:QB]
    gam = [sum(grecv[side[r] * NORB + o][0:1, 0:QB] for o in range(NORB)) for r in range(2)]
    fit0 = jnp.sum(md[...] * gam[0], axis=1, keepdims=True) + jnp.sum(off * gam[1], axis=1, keepdims=True)
    turn = jnp.broadcast_to(gam[0], (128, QB)).T
    fit1 = (jnp.sum(off * turn[:, 0:1], axis=0, keepdims=True)
            + jnp.sum(mx[...] * jnp.broadcast_to(gam[1], (128, QB)).T[:, 0:1], axis=0, keepdims=True))
    wcol = jnp.sum(off * fit1, axis=1, keepdims=True)
    wrow = jnp.sum(md[...] * fit0, axis=0, keepdims=True)
    wb[...] = jnp.broadcast_to(wrow, (128, QB)).T + wcol

    def coulomb(s, base):
        for x in range(2):
            @pl.when(2 * s + x < NG)
            def _():
                fetch(2 * s + x).wait()
        for x in range(2 * GR):
            for l0, l1 in ((0, 128), (128, 256), (256, 384), (384, NB)):
                y = bbuf[base + x // GR, x % GR, :, l0:l1] * wb[:, 0:l1 - l0]
                jp[2 * GR * s + x, :, l0:l1] = jnp.sum(y.reshape(QB // 8, 8, l1 - l0), axis=0)
        for x in range(2):
            @pl.when(2 * s + NBUF + x < NG)
            def _():
                fetch(2 * s + NBUF + x).start()

    EARLY = NST - 2 * IV

    @pl.loop(0, EARLY)
    def _(s):
        coulomb(s, 2 * lax.rem(s, 2))

    for c in (NCH - 2, NCH - 1):
        for t in range(1, NDEV):
            send(c, c % 2, t).wait_send()
    for t in range(1, NDEV):
        src = lax.rem(me + NDEV - t, NDEV)
        whole = arecv.at[src // NORB, :, pl.ds(lax.rem(src, NORB) * NCH, NCH)]
        pltpu.make_async_remote_copy(whole, whole, rsem.at[t], rsem.at[t],
                                     device_id=at(src), device_id_type=MESH).wait_recv()

    PAIRS = ((0, 0), (0, 1), (1, 0), (1, 1), (0, 2), (2, 0))

    @pl.loop(0, IV)
    def _(v):
        def decode(sd, r):
            y = arecv[side[sd], v, r // MC:r // MC + 2].astype(F32).reshape(2 * MC, QP)
            u = jnp.log(y) * (1.0 / LN2)
            return ((u + ROUND) - ROUND) * y[:, QB:QB + 1]

        for r in range(0, NORB * MP, 16):
            af[r:r + 16, :] = decode(0, r)
        af[pl.ds(pl.multiple_of(orb * MP, 8), MP), :] = own[v]
        for r in range(0, NORB * MP, 16):
            for j, x in enumerate(split3(af[r:r + 16, :])):
                aspl[j, r:r + 16, :] = x
            for j, x in enumerate(split3(decode(1, r))[:2]):
                aspl[3 + j, r:r + 16, :] = x
        t = None
        for sd in range(2):
            for i, j in PAIRS[:6 - sd]:
                x = jnp.dot(aspl[3 * sd + i], ms[j, sd * QP:(sd + 1) * QP, :], preferred_element_type=F32)
                t = x if t is None else t + x
        ts[0], ts[1], ts[2] = split3(t)
        coulomb(EARLY + 2 * v, 2 * (EARLY % 2))
        half = jnp.asarray(0.5, BF16)
        t1, t2, t3 = ts[0], ts[1], ts[2]
        s1 = lax.dot_general(t1, t1 * half, NT, preferred_element_type=F32)
        s1 = s1 + lax.dot_general(t1, t2, NT, preferred_element_type=F32)
        s1 = s1 + lax.dot_general(t1, t3, NT, preferred_element_type=F32)
        s1 = s1 + lax.dot_general(t2, t2 * half, NT, preferred_element_type=F32)
        kacc[...] += s1
        coulomb(EARLY + 2 * v + 1, 2 - 2 * (EARLY % 2))

    k = kacc[...]
    k = k + k.T
    for a in range(NAUX):
        cols = jnp.concatenate([k[:, o * MP:o * MP + MB] for o in (2 * a, 2 * a + 1)], axis=1)
        for o in range(NORB):
            kout[a * NORB + o, :, 0:OB] = -cols[o * MP:(o + 1) * MP]
    j = jnp.sum(jp[...], axis=1)
    for a in range(NAUX):
        kout[a * NORB + orb, :, 0:OB] += 2.0 * j[:, a * OB:(a + 1) * OB]

    def give(t):
        d = peer(t)
        return pltpu.make_async_remote_copy(kout.at[d], kin.at[t], ks_sem.at[t], kr_sem.at[t],
                                            device_id=at(d), device_id_type=MESH)

    for t in range(1, NDEV):
        give(t).start()
    total = kout[me]
    for t in range(1, NDEV):
        give(t).wait_recv()
        total = total + kin[t]
    out_ref[...] = total[0:MB, 0:OB]
    for t in range(1, NDEV):
        give(t).wait_send()


def fock(ints, ct, co, metric):
    vmem, hbm = pl.BlockSpec(memory_space=pltpu.VMEM), pl.BlockSpec(memory_space=pl.ANY)
    dma = pltpu.SemaphoreType.DMA
    return pl.pallas_call(
        kernel,
        name='fock',
        out_shape=jax.ShapeDtypeStruct((MB, OB), F32),
        in_specs=[hbm, vmem, vmem, vmem],
        out_specs=vmem,
        scratch_shapes=[
            pltpu.VMEM((NBUF, GR, QB, NB), F32),
            pltpu.VMEM((2 * GR, 3, QB, NB), BF16),
            pltpu.VMEM((128, NB), BF16),
            pltpu.VMEM((4, NDEV * SP, 128), F32),
            pltpu.VMEM((2, NDEV, IV, MC, QP), BF16),
            pltpu.VMEM((NAUX, IV, NORB * NCH, MC, QP), BF16),
            pltpu.VMEM((IV, MP, QP), F32),
            pltpu.VMEM((MC, QP), F32),
            pltpu.VMEM((8, QP), F32),
            pltpu.VMEM((NDEV, 8, QP), F32),
            pltpu.VMEM((QB, QB), F32),
            pltpu.VMEM((QB, QB), F32),
            pltpu.VMEM((3, 2 * QP, 2 * QP), BF16),
            pltpu.VMEM((5, NORB * MP, QP), BF16),
            pltpu.VMEM((NORB * MP, QP), F32),
            pltpu.VMEM((3, NORB * MP, 2 * QP), BF16),
            pltpu.VMEM((QB, 128), F32),
            pltpu.VMEM((MP, 8, NB), F32),
            pltpu.VMEM((NORB * MP, NORB * MP), F32),
            pltpu.VMEM((NDEV, MP, 256), F32),
            pltpu.VMEM((NDEV, MP, 256), F32),
            dma((NBUF,)), dma((2, NDEV)), dma((NDEV,)), dma((NDEV,)), dma((NDEV,)),
            dma((2,)), dma((2,)), dma((NDEV,)), dma((NDEV,)),
        ],
        compiler_params=pltpu.CompilerParams(collective_id=0, has_side_effects=True, vmem_limit_bytes=67043328),
    )(ints, ct, co, metric)


def solution(mesh):
    def local_fock(ints, metric, orbitals):
        orb = lax.axis_index('orb')
        c = orbitals[0]
        co = jnp.pad(lax.dynamic_slice_in_dim(c, orb * MB, MB, 0), ((0, MP - MB), (0, 128 - NI)))
        return fock(jnp.transpose(ints, (1, 0, 2)), c.T, co, metric)[None]

    return jax.shard_map(local_fock, mesh=mesh,
                         in_specs=(P(('sys', 'aux'), 'orb', None), P(('sys', 'aux'), None), P('sys', None, None)),
                         out_specs=P('sys', 'orb', 'aux'), check_vma=False)
```

time: 159 us -> 163 us (1.025)
  Pallas kernels: 151 us -> 159 us
  local copies, waits for them, and re-layouts: 6.74 us -> 3.27 us
    pallas_call x2 -> x1, Pallas kernels: 151 us -> 159 us  [fock(): pl.pallas_call(kernel, name='fock', out_shape=jax.ShapeDtypeStruct((MB, O...]
    dynamic_slice x1 -> x0, local copies, waits for them, and re-layouts: 3.47 us -> none  [local_fock(): mo = lax.dynamic_slice_in_dim(metric, (1 - aux) * QB, QB, 1)]
where the time goes in v3:
time: 163 us; the launch traced here: 162 us
  Pallas kernels  159 us (98%)
  local copies, waits for them, and re-layouts  3.27 us (2%)
    pallas_call x1, Pallas kernels, fock(): pl.pallas_call(kernel, name='fock', out_shape=jax.ShapeDtypeStruct((MB, O...  159 us

profile of v3, /device:TPU:0, one launch (start us, length us, event | category | flops | bytes accessed | tf_op | source)
XLA Modules:
  0.0 161.9 jit_solution(13766819711569585322)
XLA Ops:
  0.0 0.9 constant_dynamic-slice_fusion
  0.9 0.1 copy.4
  1.0 0.6 pad.4.co_ref
  1.6 158.7 %fock.1 = f32[116,232]{1,0:T(8,128)} custom-call(f32[116,464,464]{2,1,0:T(8,128)} %bitcast.b_hbm, f32[40,464]{1,0:T(8,128)} %bitcast.8, f32[120,128]{1,0:T(8,128)} %pad.4.co_ref, f32[464,928]{1,0:T(8,128)} %m_ref.1), custom_call_target="tpu_custom_call" | custom-call | tf_op jit(solution)/shard_map/fock/pallas_call | solution.py:312
  160.3 1.7 %copy.5 = f32[1,116,232]{2,0,1:T(1,128)} copy(f32[1,116,232]{2,1,0:T(8,128)} %bitcast.6) | data formatting | bytes 215296 | tf_op jit(solution)/shard_map/broadcast_in_dim | solution.py:352

commit v4 on v3

--- a/solution.py
+++ b/solution.py
@@ -38,7 +38,7 @@
 
 def kernel(b_hbm, ct_ref, co_ref, m_ref, out_ref,
            bbuf, bs, cw, abuf, sbuf, arecv, own, gbuf, gsend, grecv,
-           md, mx, ms, aspl, af, ts, wb, jp, kacc, kout, kin,
+           md, mx, ms, af, wb, jp, kacc, kout, kin,
            bsem, ssem, rsem, gs_sem, gr_sem, ms_sem, mr_sem, ks_sem, kr_sem):
     aux, orb = lax.axis_index('aux'), lax.axis_index('orb')
     me = aux * NORB + orb
@@ -53,7 +53,7 @@
 
     def fetch(g):
         slot = g % NBUF if isinstance(g, int) else lax.rem(g, NBUF)
-        return pltpu.make_async_copy(b_hbm.at[pl.ds(g * GR, GR)], bbuf.at[slot], bsem.at[slot])
+        return pltpu.make_async_copy(b_hbm.at[pl.ds(g * GR, GR)], bbuf.at[pl.ds(slot * GR, GR)], bsem.at[slot])
 
     for g in range(NBUF - 1):
         fetch(g).start()
@@ -82,24 +82,24 @@
     mfirst = mcopy(md, 0, core, {'aux': 1 - aux, 'orb': orb})
     mfirst.start()
 
-    def send(c, slot, t):
+    def send(c, t):
         d = peer(t)
-        return pltpu.make_async_remote_copy(sbuf.at[slot, d], arecv.at[aux, :, orb * NCH + c],
-                                            ssem.at[slot, t], rsem.at[t], device_id=at(d), device_id_type=MESH)
+        return pltpu.make_async_remote_copy(sbuf.at[c, d], arecv.at[aux, :, orb * NCH + c],
+                                            ssem.at[t], rsem.at[t], device_id=at(d), device_id_type=MESH)
 
     def cut(g, half):
         slot = lax.rem(g, NBUF)
         for k in range(GR):
             for r in range(0, QB, 16):
-                parts = split3(bbuf[slot, k, r:r + 16, :])
+                parts = split3(bbuf[slot * GR + k, r:r + 16, :])
                 for j in range(3):
-                    bs[half * GR + k, j, r:r + 16, :] = parts[j]
+                    bs[3 * (half * GR + k) + j, r:r + 16, 0:NB] = parts[j]
 
     def dots(half):
         for k in range(half * GR, (half + 1) * GR):
             r = None
             for j in range(3):
-                x = lax.dot_general(cw[...], bs[k, j], NT, preferred_element_type=F32)
+                x = lax.dot_general(cw[...], bs[3 * k + j, 0:QB, 0:NB], NT, preferred_element_type=F32)
                 r = x if r is None else r + x
             a2 = r[0:NI] + r[NI:2 * NI] + r[2 * NI:3 * NI]
             for v in range(IV):
@@ -110,7 +110,6 @@
     lane = lax.broadcasted_iota(jnp.int32, (MC, QP), 1)
 
     def deliver(c):
-        two = lax.rem(c, 2)
         g = gbuf[...]
         for s in range(NDEV):
             for v in range(IV):
@@ -123,22 +122,14 @@
                 up = jnp.exp2(j).astype(BF16).astype(F32)
                 down = jnp.exp2(-j).astype(BF16).astype(F32)
                 y = jnp.exp2(x * down)
-                sbuf[two, s, v] = jnp.where(lane < QB, y, up).astype(BF16)
+                sbuf[c, s, v] = jnp.where(lane < QB, y, up).astype(BF16)
         gbuf[...] = g
         for v in range(IV):
             r0 = pl.multiple_of(me * SP + v * MC, 8)
             own[v, pl.ds(pl.multiple_of(c * MC, MC), MC), :] = jnp.concatenate(
                 [abuf[lt, pl.ds(r0, MC), :] for lt in range(4)], axis=1)
         for t in range(1, NDEV):
-            send(c, two, t).start()
-
-    def reuse(c):
-        two = lax.rem(c, 2)
-
-        @pl.when(c >= 2)
-        def _():
-            for t in range(1, NDEV):
-                send(c - 2, two, t).wait_send()
+            send(c, t).start()
 
     fetch(0).wait()
     cut(jnp.int32(0), 0)
@@ -156,7 +147,6 @@
         def _():
             fetch(2 * c + 4).start()
 
-        reuse(c)
         cut(2 * c + 1, 1)
         dots(0)
         cut(2 * c + 2, 0)
@@ -165,7 +155,6 @@
 
     for g in range(NBUF):
         fetch(g).start()
-    reuse(jnp.int32(NCH - 1))
     abuf[...] = jnp.zeros_like(abuf)
     dots(0)
     deliver(jnp.int32(NCH - 1))
@@ -223,10 +212,12 @@
             @pl.when(2 * s + x < NG)
             def _():
                 fetch(2 * s + x).wait()
-        for x in range(2 * GR):
+        @pl.loop(0, 2 * GR)
+        def _(x):
             for l0, l1 in ((0, 128), (128, 256), (256, 384), (384, NB)):
-                y = bbuf[base + x // GR, x % GR, :, l0:l1] * wb[:, 0:l1 - l0]
+                y = bbuf[base * GR + x, :, l0:l1] * wb[:, 0:l1 - l0]
                 jp[2 * GR * s + x, :, l0:l1] = jnp.sum(y.reshape(QB // 8, 8, l1 - l0), axis=0)
+
         for x in range(2):
             @pl.when(2 * s + NBUF + x < NG)
             def _():
@@ -238,14 +229,13 @@
     def _(s):
         coulomb(s, 2 * lax.rem(s, 2))
 
-    for c in (NCH - 2, NCH - 1):
-        for t in range(1, NDEV):
-            send(c, c % 2, t).wait_send()
     for t in range(1, NDEV):
         src = lax.rem(me + NDEV - t, NDEV)
         whole = arecv.at[src // NORB, :, pl.ds(lax.rem(src, NORB) * NCH, NCH)]
-        pltpu.make_async_remote_copy(whole, whole, rsem.at[t], rsem.at[t],
-                                     device_id=at(src), device_id_type=MESH).wait_recv()
+        arrived = pltpu.make_async_remote_copy(whole, whole, ssem.at[t], rsem.at[t],
+                                               device_id=at(src), device_id_type=MESH)
+        arrived.wait_send()
+        arrived.wait_recv()
 
     PAIRS = ((0, 0), (0, 1), (1, 0), (1, 1), (0, 2), (2, 0))
 
@@ -261,22 +251,24 @@
         af[pl.ds(pl.multiple_of(orb * MP, 8), MP), :] = own[v]
         for r in range(0, NORB * MP, 16):
             for j, x in enumerate(split3(af[r:r + 16, :])):
-                aspl[j, r:r + 16, :] = x
+                bs[j, r:r + 16, :] = x
             for j, x in enumerate(split3(decode(1, r))[:2]):
-                aspl[3 + j, r:r + 16, :] = x
+                bs[3 + j, r:r + 16, :] = x
         t = None
         for sd in range(2):
             for i, j in PAIRS[:6 - sd]:
-                x = jnp.dot(aspl[3 * sd + i], ms[j, sd * QP:(sd + 1) * QP, :], preferred_element_type=F32)
+                x = jnp.dot(bs[3 * sd + i], ms[j, sd * QP:(sd + 1) * QP, :], preferred_element_type=F32)
                 t = x if t is None else t + x
-        ts[0], ts[1], ts[2] = split3(t)
+        for j, x in enumerate(split3(t)):
+            bs[5 + j], bs[8 + j] = x[:, 0:QP], x[:, QP:2 * QP]
         coulomb(EARLY + 2 * v, 2 * (EARLY % 2))
         half = jnp.asarray(0.5, BF16)
-        t1, t2, t3 = ts[0], ts[1], ts[2]
-        s1 = lax.dot_general(t1, t1 * half, NT, preferred_element_type=F32)
-        s1 = s1 + lax.dot_general(t1, t2, NT, preferred_element_type=F32)
-        s1 = s1 + lax.dot_general(t1, t3, NT, preferred_element_type=F32)
-        s1 = s1 + lax.dot_general(t2, t2 * half, NT, preferred_element_type=F32)
+        s1 = None
+        for b in (5, 8):
+            t1, t2, t3 = bs[b], bs[b + 1], bs[b + 2]
+            for x, y in ((t1, t1 * half), (t1, t2), (t1, t3), (t2, t2 * half)):
+                z = lax.dot_general(x, y, NT, preferred_element_type=F32)
+                s1 = z if s1 is None else s1 + z
         kacc[...] += s1
         coulomb(EARLY + 2 * v + 1, 2 - 2 * (EARLY % 2))
 
@@ -316,11 +308,11 @@
         in_specs=[hbm, vmem, vmem, vmem],
         out_specs=vmem,
         scratch_shapes=[
-            pltpu.VMEM((NBUF, GR, QB, NB), F32),
-            pltpu.VMEM((2 * GR, 3, QB, NB), BF16),
+            pltpu.VMEM((NBUF * GR, QB, NB), F32),
+            pltpu.VMEM((6 * GR, NORB * MP, QP), BF16),
             pltpu.VMEM((128, NB), BF16),
             pltpu.VMEM((4, NDEV * SP, 128), F32),
-            pltpu.VMEM((2, NDEV, IV, MC, QP), BF16),
+            pltpu.VMEM((NCH, NDEV, IV, MC, QP), BF16),
             pltpu.VMEM((NAUX, IV, NORB * NCH, MC, QP), BF16),
             pltpu.VMEM((IV, MP, QP), F32),
             pltpu.VMEM((MC, QP), F32),
@@ -329,15 +321,13 @@
             pltpu.VMEM((QB, QB), F32),
             pltpu.VMEM((QB, QB), F32),
             pltpu.VMEM((3, 2 * QP, 2 * QP), BF16),
-            pltpu.VMEM((5, NORB * MP, QP), BF16),
             pltpu.VMEM((NORB * MP, QP), F32),
-            pltpu.VMEM((3, NORB * MP, 2 * QP), BF16),
             pltpu.VMEM((QB, 128), F32),
             pltpu.VMEM((MP, 8, NB), F32),
             pltpu.VMEM((NORB * MP, NORB * MP), F32),
             pltpu.VMEM((NDEV, MP, 256), F32),
             pltpu.VMEM((NDEV, MP, 256), F32),
-            dma((NBUF,)), dma((2, NDEV)), dma((NDEV,)), dma((NDEV,)), dma((NDEV,)),
+            dma((NBUF,)), dma((NDEV,)), dma((NDEV,)), dma((NDEV,)), dma((NDEV,)),
             dma((2,)), dma((2,)), dma((NDEV,)), dma((NDEV,)),
         ],
         compiler_params=pltpu.CompilerParams(collective_id=0, has_side_effects=True, vmem_limit_bytes=67043328),

time: 163 us -> 167 us (1.025)
  Pallas kernels: 159 us -> 163 us
    pallas_call x1, Pallas kernels: 159 us -> 163 us  [fock(): pl.pallas_call(kernel, name='fock', out_shape=jax.ShapeDtypeStruct((MB, O...]
where the time goes in v4:
time: 167 us; the launch traced here: 166 us
  Pallas kernels  163 us (98%)
  local copies, waits for them, and re-layouts  3.27 us (2%)
    pallas_call x1, Pallas kernels, fock(): pl.pallas_call(kernel, name='fock', out_shape=jax.ShapeDtypeStruct((MB, O...  163 us

profile of v4, /device:TPU:0, one launch (start us, length us, event | category | flops | bytes accessed | tf_op | source)
XLA Modules:
  0.0 166.4 jit_solution(15707443917158132812)
XLA Ops:
  0.0 0.9 constant_dynamic-slice_fusion
  0.9 0.1 copy.4
  1.0 0.6 pad.4.co_ref
  1.6 163.2 %fock.1 = f32[116,232]{1,0:T(8,128)} custom-call(f32[116,464,464]{2,1,0:T(8,128)} %bitcast.b_hbm, f32[40,464]{1,0:T(8,128)} %bitcast.8, f32[120,128]{1,0:T(8,128)} %pad.4.co_ref, f32[464,928]{1,0:T(8,128)} %m_ref.1), custom_call_target="tpu_custom_call" | custom-call | tf_op jit(solution)/shard_map/fock/pallas_call | solution.py:304
  164.8 1.7 %copy.5 = f32[1,116,232]{2,0,1:T(1,128)} copy(f32[1,116,232]{2,1,0:T(8,128)} %bitcast.6) | data formatting | bytes 215296 | tf_op jit(solution)/shard_map/broadcast_in_dim | solution.py:342

commit v5 on v4

--- a/solution.py
+++ b/solution.py
@@ -45,11 +45,26 @@
     core = lax.rem(orb, 2)
     side = (aux, 1 - aux)
 
-    def at(d):
-        return {'aux': d // NORB, 'orb': lax.rem(d, NORB)}
-
-    def peer(t):
-        return lax.rem(me + t, NDEV)
+    chip = orb // 2
+
+    STEPS = tuple((core, 1 - core, k) for k in range(2)) + tuple((1 - core, core, k) for k in range(2)) \
+        + ((1, 1, 0), (1, 1, 1), (0, 0, 1))
+
+    def peer(n):
+        y, x, k = STEPS[n]
+        return lax.rem(aux + y, 2), 2 * lax.rem(chip + x, 2) + lax.rem(core + k, 2)
+
+    def name(n):
+        y, x, k = STEPS[n]
+        return 4 * y + 2 * x + k
+
+    def at(n):
+        a, o = peer(n)
+        return {'aux': a, 'orb': o}
+
+    def index(n):
+        a, o = peer(n)
+        return a * NORB + o
 
     def fetch(g):
         slot = g % NBUF if isinstance(g, int) else lax.rem(g, NBUF)
@@ -59,8 +74,8 @@
         fetch(g).start()
 
     barrier = pltpu.get_barrier_semaphore()
-    for t in range(1, NDEV):
-        pl.semaphore_signal(barrier, inc=1, device_id=at(peer(t)), device_id_type=MESH)
+    for t in range(NDEV - 1):
+        pl.semaphore_signal(barrier, inc=1, device_id=at(t), device_id_type=MESH)
 
     for a in range(NAUX):
         @pl.when(aux == a)
@@ -83,9 +98,8 @@
     mfirst.start()
 
     def send(c, t):
-        d = peer(t)
-        return pltpu.make_async_remote_copy(sbuf.at[c, d], arecv.at[aux, :, orb * NCH + c],
-                                            ssem.at[t], rsem.at[t], device_id=at(d), device_id_type=MESH)
+        return pltpu.make_async_remote_copy(sbuf.at[c, index(t)], arecv.at[aux, :, orb * NCH + c],
+                                            ssem.at[name(t)], rsem.at[name(t)], device_id=at(t), device_id_type=MESH)
 
     def cut(g, half):
         slot = lax.rem(g, NBUF)
@@ -128,7 +142,7 @@
             r0 = pl.multiple_of(me * SP + v * MC, 8)
             own[v, pl.ds(pl.multiple_of(c * MC, MC), MC), :] = jnp.concatenate(
                 [abuf[lt, pl.ds(r0, MC), :] for lt in range(4)], axis=1)
-        for t in range(1, NDEV):
+        for t in range(NDEV - 1):
             send(c, t).start()
 
     fetch(0).wait()
@@ -162,10 +176,10 @@
     gsend[...] = jnp.broadcast_to(jnp.sum(gbuf[...], axis=0, keepdims=True), (8, QP))
 
     def gcopy(t):
-        return pltpu.make_async_remote_copy(gsend, grecv.at[me], gs_sem.at[t], gr_sem.at[t],
-                                            device_id=at(peer(t)), device_id_type=MESH)
-
-    for t in range(1, NDEV):
+        return pltpu.make_async_remote_copy(gsend, grecv.at[me], gs_sem.at[name(t)], gr_sem.at[name(t)],
+                                            device_id=at(t), device_id_type=MESH)
+
+    for t in range(NDEV - 1):
         gcopy(t).start()
     grecv[me] = gsend[...]
 
@@ -193,10 +207,9 @@
     parts_of(mx[...], 1, 1)
     kacc[...] = jnp.zeros_like(kacc)
 
-    for t in range(1, NDEV):
-        src = lax.rem(me + NDEV - t, NDEV)
-        pltpu.make_async_remote_copy(gsend, grecv.at[src], gs_sem.at[t], gr_sem.at[t],
-                                     device_id=at(src), device_id_type=MESH).wait()
+    for t in range(NDEV - 1):
+        pltpu.make_async_remote_copy(gsend, grecv.at[index(t)], gs_sem.at[name(t)], gr_sem.at[name(t)],
+                                     device_id=at(t), device_id_type=MESH).wait()
     off = af[0:QB, 0:QB]
     gam = [sum(grecv[side[r] * NORB + o][0:1, 0:QB] for o in range(NORB)) for r in range(2)]
     fit0 = jnp.sum(md[...] * gam[0], axis=1, keepdims=True) + jnp.sum(off * gam[1], axis=1, keepdims=True)
@@ -229,11 +242,11 @@
     def _(s):
         coulomb(s, 2 * lax.rem(s, 2))
 
-    for t in range(1, NDEV):
-        src = lax.rem(me + NDEV - t, NDEV)
-        whole = arecv.at[src // NORB, :, pl.ds(lax.rem(src, NORB) * NCH, NCH)]
-        arrived = pltpu.make_async_remote_copy(whole, whole, ssem.at[t], rsem.at[t],
-                                               device_id=at(src), device_id_type=MESH)
+    for t in range(NDEV - 1):
+        a, o = peer(t)
+        whole = arecv.at[a, :, pl.ds(o * NCH, NCH)]
+        arrived = pltpu.make_async_remote_copy(whole, whole, ssem.at[name(t)], rsem.at[name(t)],
+                                               device_id=at(t), device_id_type=MESH)
         arrived.wait_send()
         arrived.wait_recv()
 
@@ -283,18 +296,17 @@
         kout[a * NORB + orb, :, 0:OB] += 2.0 * j[:, a * OB:(a + 1) * OB]
 
     def give(t):
-        d = peer(t)
-        return pltpu.make_async_remote_copy(kout.at[d], kin.at[t], ks_sem.at[t], kr_sem.at[t],
-                                            device_id=at(d), device_id_type=MESH)
-
-    for t in range(1, NDEV):
+        return pltpu.make_async_remote_copy(kout.at[index(t)], kin.at[name(t)], ks_sem.at[name(t)], kr_sem.at[name(t)],
+                                            device_id=at(t), device_id_type=MESH)
+
+    for t in range(NDEV - 1):
         give(t).start()
     total = kout[me]
-    for t in range(1, NDEV):
+    for t in range(NDEV - 1):
         give(t).wait_recv()
-        total = total + kin[t]
+        total = total + kin[name(t)]
     out_ref[...] = total[0:MB, 0:OB]
-    for t in range(1, NDEV):
+    for t in range(NDEV - 1):
         give(t).wait_send()
 
 

time: 167 us -> 167 us (level)
  no operation moved by 1% of the time
where the time goes in v5:
time: 167 us
  Pallas kernels  164 us (98%)
  local copies, waits for them, and re-layouts  3.27 us (2%)
    pallas_call x1, Pallas kernels, fock(): pl.pallas_call(kernel, name='fock', out_shape=jax.ShapeDtypeStruct((MB, O...  164 us

profile of v5, /device:TPU:0, one launch (start us, length us, event | category | flops | bytes accessed | tf_op | source)
XLA Modules:
  0.0 167.1 jit_solution(6834595936298764103)
XLA Ops:
  0.0 0.9 constant_dynamic-slice_fusion
  0.9 0.1 copy.4
  1.0 0.6 pad.4.co_ref
  1.6 163.8 %fock.1 = f32[116,232]{1,0:T(8,128)} custom-call(f32[116,464,464]{2,1,0:T(8,128)} %bitcast.b_hbm, f32[40,464]{1,0:T(8,128)} %bitcast.8, f32[120,128]{1,0:T(8,128)} %pad.4.co_ref, f32[464,928]{1,0:T(8,128)} %m_ref.1), custom_call_target="tpu_custom_call" | custom-call | tf_op jit(solution)/shard_map/fock/pallas_call | solution.py:316
  165.4 1.7 %copy.5 = f32[1,116,232]{2,0,1:T(1,128)} copy(f32[1,116,232]{2,1,0:T(8,128)} %bitcast.6) | data formatting | bytes 215296 | tf_op jit(solution)/shard_map/broadcast_in_dim | solution.py:354

commit v6 on v5

--- a/solution.py
+++ b/solution.py
@@ -23,6 +23,7 @@
 GR = 4
 NG = MB // GR
 NBUF = 4
+GROUPS = (2, 2, 3, 3, 3, 2)
 NST = (NG + 1) // 2
 OB = NB // NAUX
 HQ = QB // 2
@@ -97,8 +98,8 @@
     mfirst = mcopy(md, 0, core, {'aux': 1 - aux, 'orb': orb})
     mfirst.start()
 
-    def send(c, t):
-        return pltpu.make_async_remote_copy(sbuf.at[c, index(t)], arecv.at[aux, :, orb * NCH + c],
+    def send(c, n, t):
+        return pltpu.make_async_remote_copy(sbuf.at[index(t), :, c:c + n], arecv.at[aux, :, pl.ds(orb * NCH + c, n)],
                                             ssem.at[name(t)], rsem.at[name(t)], device_id=at(t), device_id_type=MESH)
 
     def cut(g, half):
@@ -136,14 +137,17 @@
                 up = jnp.exp2(j).astype(BF16).astype(F32)
                 down = jnp.exp2(-j).astype(BF16).astype(F32)
                 y = jnp.exp2(x * down)
-                sbuf[c, s, v] = jnp.where(lane < QB, y, up).astype(BF16)
+                sbuf[s, v, c] = jnp.where(lane < QB, y, up).astype(BF16)
         gbuf[...] = g
         for v in range(IV):
             r0 = pl.multiple_of(me * SP + v * MC, 8)
             own[v, pl.ds(pl.multiple_of(c * MC, MC), MC), :] = jnp.concatenate(
                 [abuf[lt, pl.ds(r0, MC), :] for lt in range(4)], axis=1)
-        for t in range(NDEV - 1):
-            send(c, t).start()
+        for e in range(len(GROUPS)):
+            @pl.when(c == sum(GROUPS[:e + 1]) - 1)
+            def _():
+                for t in range(NDEV - 1):
+                    send(sum(GROUPS[:e]), GROUPS[e], t).start()
 
     fetch(0).wait()
     cut(jnp.int32(0), 0)
@@ -324,7 +328,7 @@
             pltpu.VMEM((6 * GR, NORB * MP, QP), BF16),
             pltpu.VMEM((128, NB), BF16),
             pltpu.VMEM((4, NDEV * SP, 128), F32),
-            pltpu.VMEM((NCH, NDEV, IV, MC, QP), BF16),
+            pltpu.VMEM((NDEV, IV, NCH, MC, QP), BF16),
             pltpu.VMEM((NAUX, IV, NORB * NCH, MC, QP), BF16),
             pltpu.VMEM((IV, MP, QP), F32),
             pltpu.VMEM((MC, QP), F32),

time: 167 us -> 173 us (1.036)
  Pallas kernels: 164 us -> 170 us
    pallas_call x1, Pallas kernels: 164 us -> 170 us  [fock(): pl.pallas_call(kernel, name='fock', out_shape=jax.ShapeDtypeStruct((MB, O...]
where the time goes in v6:
time: 173 us
  Pallas kernels  170 us (98%)
  local copies, waits for them, and re-layouts  3.27 us (2%)
    pallas_call x1, Pallas kernels, fock(): pl.pallas_call(kernel, name='fock', out_shape=jax.ShapeDtypeStruct((MB, O...  170 us

profile of v6, /device:TPU:0, one launch (start us, length us, event | category | flops | bytes accessed | tf_op | source)
XLA Modules:
  0.0 172.9 jit_solution(2262200236645170938)
XLA Ops:
  0.0 0.9 constant_dynamic-slice_fusion
  0.9 0.1 copy.4
  1.0 0.6 pad.4.co_ref
  1.6 169.6 %fock.1 = f32[116,232]{1,0:T(8,128)} custom-call(f32[116,464,464]{2,1,0:T(8,128)} %bitcast.b_hbm, f32[40,464]{1,0:T(8,128)} %bitcast.8, f32[120,128]{1,0:T(8,128)} %pad.4.co_ref, f32[464,928]{1,0:T(8,128)} %m_ref.1), custom_call_target="tpu_custom_call" | custom-call | tf_op jit(solution)/shard_map/fock/pallas_call | solution.py:320
  171.2 1.7 copy.5

commit v7 on v5

--- a/solution.py
+++ b/solution.py
@@ -23,6 +23,7 @@
 GR = 4
 NG = MB // GR
 NBUF = 4
+MTURN = 6
 NST = (NG + 1) // 2
 OB = NB // NAUX
 HQ = QB // 2
@@ -148,8 +149,15 @@
     fetch(0).wait()
     cut(jnp.int32(0), 0)
 
+    msecond = mcopy(mx, 1, core, {'orb': orb + 1 - 2 * core})
+
     @pl.loop(0, NCH - 1)
     def _(c):
+        @pl.when(c == MTURN)
+        def _():
+            mfirst.wait()
+            msecond.start()
+
         fetch(2 * c + 1).wait()
         fetch(2 * c + 2).wait()
 
@@ -182,10 +190,6 @@
     for t in range(NDEV - 1):
         gcopy(t).start()
     grecv[me] = gsend[...]
-
-    mfirst.wait()
-    msecond = mcopy(mx, 1, core, {'orb': orb + 1 - 2 * core})
-    msecond.start()
 
     ms[...] = jnp.zeros_like(ms)
 
@@ -206,6 +210,30 @@
     mcopy(mx, 1, 1 - core, {'orb': orb + 1 - 2 * core}).wait_recv()
     parts_of(mx[...], 1, 1)
     kacc[...] = jnp.zeros_like(kacc)
+
+    def coulomb(s, base):
+        for x in range(2):
+            @pl.when(2 * s + x < NG)
+            def _():
+                fetch(2 * s + x).wait()
+        @pl.loop(0, 2 * GR)
+        def _(x):
+            for l0, l1 in ((0, 128), (128, 256), (256, 384), (384, NB)):
+                y = bbuf[base * GR + x, :, l0:l1] * wb[:, 0:l1 - l0]
+                jp[2 * GR * s + x, :, l0:l1] = jnp.sum(y.reshape(QB // 8, 8, l1 - l0), axis=0)
+
+        for x in range(2):
+            @pl.when(2 * s + NBUF + x < NG)
+            def _():
+                fetch(2 * s + NBUF + x).start()
+
+    for t in range(NDEV - 1):
+        a, o = peer(t)
+        whole = arecv.at[a, :, pl.ds(o * NCH, NCH)]
+        arrived = pltpu.make_async_remote_copy(whole, whole, ssem.at[name(t)], rsem.at[name(t)],
+                                               device_id=at(t), device_id_type=MESH)
+        arrived.wait_send()
+        arrived.wait_recv()
 
     for t in range(NDEV - 1):
         pltpu.make_async_remote_copy(gsend, grecv.at[index(t)], gs_sem.at[name(t)], gr_sem.at[name(t)],
@@ -219,36 +247,6 @@
     wcol = jnp.sum(off * fit1, axis=1, keepdims=True)
     wrow = jnp.sum(md[...] * fit0, axis=0, keepdims=True)
     wb[...] = jnp.broadcast_to(wrow, (128, QB)).T + wcol
-
-    def coulomb(s, base):
-        for x in range(2):
-            @pl.when(2 * s + x < NG)
-            def _():
-                fetch(2 * s + x).wait()
-        @pl.loop(0, 2 * GR)
-        def _(x):
-            for l0, l1 in ((0, 128), (128, 256), (256, 384), (384, NB)):
-                y = bbuf[base * GR + x, :, l0:l1] * wb[:, 0:l1 - l0]
-                jp[2 * GR * s + x, :, l0:l1] = jnp.sum(y.reshape(QB // 8, 8, l1 - l0), axis=0)
-
-        for x in range(2):
-            @pl.when(2 * s + NBUF + x < NG)
-            def _():
-                fetch(2 * s + NBUF + x).start()
-
-    EARLY = NST - 2 * IV
-
-    @pl.loop(0, EARLY)
-    def _(s):
-        coulomb(s, 2 * lax.rem(s, 2))
-
-    for t in range(NDEV - 1):
-        a, o = peer(t)
-        whole = arecv.at[a, :, pl.ds(o * NCH, NCH)]
-        arrived = pltpu.make_async_remote_copy(whole, whole, ssem.at[name(t)], rsem.at[name(t)],
-                                               device_id=at(t), device_id_type=MESH)
-        arrived.wait_send()
-        arrived.wait_recv()
 
     PAIRS = ((0, 0), (0, 1), (1, 0), (1, 1), (0, 2), (2, 0))
 
@@ -274,7 +272,7 @@
                 t = x if t is None else t + x
         for j, x in enumerate(split3(t)):
             bs[5 + j], bs[8 + j] = x[:, 0:QP], x[:, QP:2 * QP]
-        coulomb(EARLY + 2 * v, 2 * (EARLY % 2))
+        coulomb(3 * v, 2 * lax.rem(v, 2))
         half = jnp.asarray(0.5, BF16)
         s1 = None
         for b in (5, 8):
@@ -283,7 +281,8 @@
                 z = lax.dot_general(x, y, NT, preferred_element_type=F32)
                 s1 = z if s1 is None else s1 + z
         kacc[...] += s1
-        coulomb(EARLY + 2 * v + 1, 2 - 2 * (EARLY % 2))
+        coulomb(3 * v + 1, 2 - 2 * lax.rem(v, 2))
+        coulomb(3 * v + 2, 2 * lax.rem(v, 2))
 
     k = kacc[...]
     k = k + k.T

time: 167 us -> 163 us (0.976)
  Pallas kernels: 164 us -> 159 us
    pallas_call x1, Pallas kernels: 164 us -> 159 us  [fock(): pl.pallas_call(kernel, name='fock', out_shape=jax.ShapeDtypeStruct((MB, O...]
where the time goes in v7:
time: 163 us; the launch traced here: 162 us
  Pallas kernels  159 us (98%)
  local copies, waits for them, and re-layouts  3.27 us (2%)
    pallas_call x1, Pallas kernels, fock(): pl.pallas_call(kernel, name='fock', out_shape=jax.ShapeDtypeStruct((MB, O...  159 us

profile of v7, /device:TPU:0, one launch (start us, length us, event | category | flops | bytes accessed | tf_op | source)
XLA Modules:
  0.0 162.5 jit_solution(814536072805979465)
XLA Ops:
  0.0 0.9 constant_dynamic-slice_fusion
  0.9 0.1 copy.4
  1.0 0.6 pad.4.co_ref
  1.6 159.2 %fock.1 = f32[116,232]{1,0:T(8,128)} custom-call(f32[116,464,464]{2,1,0:T(8,128)} %bitcast.b_hbm, f32[40,464]{1,0:T(8,128)} %bitcast.8, f32[120,128]{1,0:T(8,128)} %pad.4.co_ref, f32[464,928]{1,0:T(8,128)} %m_ref.1), custom_call_target="tpu_custom_call" | custom-call | tf_op jit(solution)/shard_map/fock/pallas_call | solution.py:315
  160.8 1.7 %copy.5 = f32[1,116,232]{2,0,1:T(1,128)} copy(f32[1,116,232]{2,1,0:T(8,128)} %bitcast.6) | data formatting | bytes 215296 | tf_op jit(solution)/shard_map/broadcast_in_dim | solution.py:353

commit v8 on v7

--- a/solution.py
+++ b/solution.py
@@ -23,6 +23,7 @@
 GR = 4
 NG = MB // GR
 NBUF = 4
+LAG = 4
 MTURN = 6
 NST = (NG + 1) // 2
 OB = NB // NAUX
@@ -40,7 +41,7 @@
 def kernel(b_hbm, ct_ref, co_ref, m_ref, out_ref,
            bbuf, bs, cw, abuf, sbuf, arecv, own, gbuf, gsend, grecv,
            md, mx, ms, af, wb, jp, kacc, kout, kin,
-           bsem, ssem, rsem, gs_sem, gr_sem, ms_sem, mr_sem, ks_sem, kr_sem):
+           bsem, ssem, rsem, gs_sem, gr_sem, ms_sem, mr_sem, ks_sem, kr_sem, rbuf, lsem, fsem):
     aux, orb = lax.axis_index('aux'), lax.axis_index('orb')
     me = aux * NORB + orb
     core = lax.rem(orb, 2)
@@ -101,6 +102,26 @@
     def send(c, t):
         return pltpu.make_async_remote_copy(sbuf.at[c, index(t)], arecv.at[aux, :, orb * NCH + c],
                                             ssem.at[name(t)], rsem.at[name(t)], device_id=at(t), device_id_type=MESH)
+
+    def relay(c, k):
+        o = 2 * chip + lax.rem(core + k, 2)
+        d = (1 - aux) * NORB + 2 * (1 - chip) + lax.rem(core + k, 2)
+        return pltpu.make_async_remote_copy(sbuf.at[c, d], rbuf.at[core, c], ssem.at[6 + k], lsem.at[core, c],
+                                            device_id={'aux': 1 - aux, 'orb': o}, device_id_type=MESH)
+
+    def onward(c, k):
+        return pltpu.make_async_remote_copy(
+            rbuf.at[k, c], arecv.at[1 - aux, :, (2 * chip + k) * NCH + c], fsem.at[k],
+            rsem.at[6 + lax.rem(k + core, 2)], device_id={'orb': 2 * (1 - chip) + core}, device_id_type=MESH)
+
+    def arrived_relay(c, k):
+        return pltpu.make_async_remote_copy(rbuf.at[k, c], rbuf.at[k, c], fsem.at[k], lsem.at[k, c],
+                                            device_id={'orb': orb}, device_id_type=MESH)
+
+    def pass_on(c):
+        for k in range(2):
+            arrived_relay(c, k).wait_recv()
+            onward(c, k).start()
 
     def cut(g, half):
         slot = lax.rem(g, NBUF)
@@ -143,7 +164,9 @@
             r0 = pl.multiple_of(me * SP + v * MC, 8)
             own[v, pl.ds(pl.multiple_of(c * MC, MC), MC), :] = jnp.concatenate(
                 [abuf[lt, pl.ds(r0, MC), :] for lt in range(4)], axis=1)
-        for t in range(NDEV - 1):
+        for k in range(2):
+            relay(c, k).start()
+        for t in (0, 1, 2, 3, 6):
             send(c, t).start()
 
     fetch(0).wait()
@@ -174,6 +197,10 @@
         cut(2 * c + 2, 0)
         dots(1)
         deliver(c)
+
+        @pl.when(c >= LAG)
+        def _():
+            pass_on(c - LAG)
 
     for g in range(NBUF):
         fetch(g).start()
@@ -227,6 +254,10 @@
             def _():
                 fetch(2 * s + NBUF + x).start()
 
+    @pl.loop(NCH - 1 - LAG, NCH)
+    def _(c):
+        pass_on(c)
+
     for t in range(NDEV - 1):
         a, o = peer(t)
         whole = arecv.at[a, :, pl.ds(o * NCH, NCH)]
@@ -234,6 +265,10 @@
                                                device_id=at(t), device_id_type=MESH)
         arrived.wait_send()
         arrived.wait_recv()
+    for k in range(2):
+        whole = rbuf.at[k]
+        pltpu.make_async_remote_copy(whole, whole, fsem.at[k], fsem.at[k],
+                                     device_id={'orb': orb}, device_id_type=MESH).wait_send()
 
     for t in range(NDEV - 1):
         pltpu.make_async_remote_copy(gsend, grecv.at[index(t)], gs_sem.at[name(t)], gr_sem.at[name(t)],
@@ -340,6 +375,7 @@
             pltpu.VMEM((NDEV, MP, 256), F32),
             dma((NBUF,)), dma((NDEV,)), dma((NDEV,)), dma((NDEV,)), dma((NDEV,)),
             dma((2,)), dma((2,)), dma((NDEV,)), dma((NDEV,)),
+            pltpu.VMEM((2, NCH, IV, MC, QP), BF16), dma((2, NCH)), dma((2,)),
         ],
         compiler_params=pltpu.CompilerParams(collective_id=0, has_side_effects=True, vmem_limit_bytes=67043328),
     )(ints, ct, co, metric)

time: 163 us -> 169 us (1.037)
  Pallas kernels: 159 us -> 165 us
    pallas_call x1, Pallas kernels: 159 us -> 165 us  [fock(): pl.pallas_call(kernel, name='fock', out_shape=jax.ShapeDtypeStruct((MB, O...]
where the time goes in v8:
time: 169 us
  Pallas kernels  165 us (98%)
  local copies, waits for them, and re-layouts  3.27 us (2%)
    pallas_call x1, Pallas kernels, fock(): pl.pallas_call(kernel, name='fock', out_shape=jax.ShapeDtypeStruct((MB, O...  165 us

profile of v8, /device:TPU:0, one launch (start us, length us, event | category | flops | bytes accessed | tf_op | source)
XLA Modules:
  0.0 168.6 jit_solution(12545412881057398845)
XLA Ops:
  0.0 0.9 constant_dynamic-slice_fusion
  0.9 0.1 copy.4
  1.0 0.6 pad.4.co_ref
  1.6 165.3 %fock.1 = f32[116,232]{1,0:T(8,128)} custom-call(f32[116,464,464]{2,1,0:T(8,128)} %bitcast.b_hbm, f32[40,464]{1,0:T(8,128)} %bitcast.8, f32[120,128]{1,0:T(8,128)} %pad.4.co_ref, f32[464,928]{1,0:T(8,128)} %m_ref.1), custom_call_target="tpu_custom_call" | custom-call | tf_op jit(solution)/shard_map/fock/pallas_call | solution.py:350
  166.9 1.7 copy.5

commit v9 on v7

--- a/solution.py
+++ b/solution.py
@@ -87,7 +87,7 @@
     gbuf[...] = jnp.zeros_like(gbuf)
     c1, c2, c3 = split3(ct_ref[...])
     cw[...] = jnp.concatenate(
-        [c1.astype(F32), c2.astype(F32), c3.astype(F32), jnp.zeros((8, NB), F32)], axis=0).astype(BF16)
+        [c1.astype(F32), c2.astype(F32), c3.astype(F32), jnp.zeros((8, NB), F32)], axis=0).T.astype(BF16)
 
     pl.semaphore_wait(barrier, NDEV - 1)
 
@@ -114,8 +114,9 @@
         for k in range(half * GR, (half + 1) * GR):
             r = None
             for j in range(3):
-                x = lax.dot_general(cw[...], bs[3 * k + j, 0:QB, 0:NB], NT, preferred_element_type=F32)
+                x = jnp.dot(bs[3 * k + j, 0:QB, 0:NB], cw[...], preferred_element_type=F32)
                 r = x if r is None else r + x
+            r = r.T
             a2 = r[0:NI] + r[NI:2 * NI] + r[2 * NI:3 * NI]
             for v in range(IV):
                 for lt in range(4):
@@ -321,7 +322,7 @@
         scratch_shapes=[
             pltpu.VMEM((NBUF * GR, QB, NB), F32),
             pltpu.VMEM((6 * GR, NORB * MP, QP), BF16),
-            pltpu.VMEM((128, NB), BF16),
+            pltpu.VMEM((NB, 128), BF16),
             pltpu.VMEM((4, NDEV * SP, 128), F32),
             pltpu.VMEM((NCH, NDEV, IV, MC, QP), BF16),
             pltpu.VMEM((NAUX, IV, NORB * NCH, MC, QP), BF16),

time: 163 us -> 157 us (0.963)
  Pallas kernels: 159 us -> 153 us
    pallas_call x1, Pallas kernels: 159 us -> 153 us  [fock(): pl.pallas_call(kernel, name='fock', out_shape=jax.ShapeDtypeStruct((MB, O...]
where the time goes in v9:
time: 157 us
  Pallas kernels  153 us (97%)
  local copies, waits for them, and re-layouts  3.27 us (2%)
    pallas_call x1, Pallas kernels, fock(): pl.pallas_call(kernel, name='fock', out_shape=jax.ShapeDtypeStruct((MB, O...  153 us

profile of v9, /device:TPU:0, one launch (start us, length us, event | category | flops | bytes accessed | tf_op | source)
XLA Modules:
  0.0 156.6 jit_solution(16744813881638164198)
XLA Ops:
  0.0 0.9 constant_dynamic-slice_fusion
  0.9 0.1 copy.4
  1.0 0.6 pad.4.co_ref
  1.6 153.3 %fock.1 = f32[116,232]{1,0:T(8,128)} custom-call(f32[116,464,464]{2,1,0:T(8,128)} %bitcast.b_hbm, f32[40,464]{1,0:T(8,128)} %bitcast.8, f32[120,128]{1,0:T(8,128)} %pad.4.co_ref, f32[464,928]{1,0:T(8,128)} %m_ref.1), custom_call_target="tpu_custom_call" | custom-call | tf_op jit(solution)/shard_map/fock/pallas_call | solution.py:316
  154.9 1.7 %copy.5 = f32[1,116,232]{2,0,1:T(1,128)} copy(f32[1,116,232]{2,1,0:T(8,128)} %bitcast.6) | data formatting | bytes 215296 | tf_op jit(solution)/shard_map/broadcast_in_dim | solution.py:354

commit v10 on v9

--- a/solution.py
+++ b/solution.py
@@ -102,16 +102,16 @@
         return pltpu.make_async_remote_copy(sbuf.at[c, index(t)], arecv.at[aux, :, orb * NCH + c],
                                             ssem.at[name(t)], rsem.at[name(t)], device_id=at(t), device_id_type=MESH)
 
-    def cut(g, half):
+    def cut(g, ks):
         slot = lax.rem(g, NBUF)
-        for k in range(GR):
+        for k in ks:
             for r in range(0, QB, 16):
                 parts = split3(bbuf[slot * GR + k, r:r + 16, :])
                 for j in range(3):
-                    bs[3 * (half * GR + k) + j, r:r + 16, 0:NB] = parts[j]
-
-    def dots(half):
-        for k in range(half * GR, (half + 1) * GR):
+                    bs[3 * k + j, r:r + 16, 0:NB] = parts[j]
+
+    def dots(half, ks):
+        for k in ks:
             r = None
             for j in range(3):
                 x = jnp.dot(bs[3 * k + j, 0:QB, 0:NB], cw[...], preferred_element_type=F32)
@@ -121,7 +121,7 @@
             for v in range(IV):
                 for lt in range(4):
                     l0, l1 = lt * 128, min(lt * 128 + 128, QB)
-                    abuf[lt, pl.ds(v * MC + k, NDEV, stride=SP), 0:l1 - l0] = a2[8 * v:8 * v + 8, l0:l1]
+                    abuf[lt, pl.ds(v * MC + half * GR + k, NDEV, stride=SP), 0:l1 - l0] = a2[8 * v:8 * v + 8, l0:l1]
 
     lane = lax.broadcasted_iota(jnp.int32, (MC, QP), 1)
 
@@ -148,7 +148,7 @@
             send(c, t).start()
 
     fetch(0).wait()
-    cut(jnp.int32(0), 0)
+    cut(jnp.int32(0), range(GR))
 
     msecond = mcopy(mx, 1, core, {'orb': orb + 1 - 2 * core})
 
@@ -170,16 +170,16 @@
         def _():
             fetch(2 * c + 4).start()
 
-        cut(2 * c + 1, 1)
-        dots(0)
-        cut(2 * c + 2, 0)
-        dots(1)
+        for half in range(2):
+            for k in range(GR):
+                dots(half, (k,))
+                cut(2 * c + 1 + half, (k,))
         deliver(c)
 
     for g in range(NBUF):
         fetch(g).start()
     abuf[...] = jnp.zeros_like(abuf)
-    dots(0)
+    dots(0, range(GR))
     deliver(jnp.int32(NCH - 1))
 
     gsend[...] = jnp.broadcast_to(jnp.sum(gbuf[...], axis=0, keepdims=True), (8, QP))
@@ -321,7 +321,7 @@
         out_specs=vmem,
         scratch_shapes=[
             pltpu.VMEM((NBUF * GR, QB, NB), F32),
-            pltpu.VMEM((6 * GR, NORB * MP, QP), BF16),
+            pltpu.VMEM((3 * GR, NORB * MP, QP), BF16),
             pltpu.VMEM((NB, 128), BF16),
             pltpu.VMEM((4, NDEV * SP, 128), F32),
             pltpu.VMEM((NCH, NDEV, IV, MC, QP), BF16),

time: 157 us -> 159 us (1.013)
  Pallas kernels: 153 us -> 155 us
    pallas_call x1, Pallas kernels: 153 us -> 155 us  [fock(): pl.pallas_call(kernel, name='fock', out_shape=jax.ShapeDtypeStruct((MB, O...]
where the time goes in v10:
time: 159 us
  Pallas kernels  155 us (97%)
  local copies, waits for them, and re-layouts  3.27 us (2%)
    pallas_call x1, Pallas kernels, fock(): pl.pallas_call(kernel, name='fock', out_shape=jax.ShapeDtypeStruct((MB, O...  155 us

profile of v10, /device:TPU:0, one launch (start us, length us, event | category | flops | bytes accessed | tf_op | source)
XLA Modules:
  0.0 158.6 jit_solution(13104211402482409754)
XLA Ops:
  0.0 0.9 constant_dynamic-slice_fusion
  0.9 0.1 copy.4
  1.0 0.6 pad.4.co_ref
  1.6 155.3 %fock.1 = f32[116,232]{1,0:T(8,128)} custom-call(f32[116,464,464]{2,1,0:T(8,128)} %bitcast.b_hbm, f32[40,464]{1,0:T(8,128)} %bitcast.8, f32[120,128]{1,0:T(8,128)} %pad.4.co_ref, f32[464,928]{1,0:T(8,128)} %m_ref.1), custom_call_target="tpu_custom_call" | custom-call | tf_op jit(solution)/shard_map/fock/pallas_call | solution.py:316
  156.9 1.7 %copy.5 = f32[1,116,232]{2,0,1:T(1,128)} copy(f32[1,116,232]{2,1,0:T(8,128)} %bitcast.6) | data formatting | bytes 215296 | tf_op jit(solution)/shard_map/broadcast_in_dim | solution.py:354

commit v11 on v9

--- a/solution.py
+++ b/solution.py
@@ -88,6 +88,22 @@
     c1, c2, c3 = split3(ct_ref[...])
     cw[...] = jnp.concatenate(
         [c1.astype(F32), c2.astype(F32), c3.astype(F32), jnp.zeros((8, NB), F32)], axis=0).T.astype(BF16)
+
+    ms[...] = jnp.zeros_like(ms)
+
+    def parts_of(x, r, s):
+        parts = split3(x)
+        for j in range(3):
+            ms[j, r * QP:r * QP + QB, s * QP:s * QP + QB] = parts[j]
+
+    parts_of(md[...], 0, 0)
+    for a in range(NAUX):
+        @pl.when(aux == a)
+        def _():
+            off = m_ref[:, (1 - a) * QB:(2 - a) * QB]
+            af[0:QB, 0:QB] = off
+    parts_of(af[0:QB, 0:QB], 0, 1)
+    parts_of(af[0:QB, 0:QB].T, 1, 0)
 
     pl.semaphore_wait(barrier, NDEV - 1)
 
@@ -192,21 +208,6 @@
         gcopy(t).start()
     grecv[me] = gsend[...]
 
-    ms[...] = jnp.zeros_like(ms)
-
-    def parts_of(x, r, s):
-        parts = split3(x)
-        for j in range(3):
-            ms[j, r * QP:r * QP + QB, s * QP:s * QP + QB] = parts[j]
-
-    parts_of(md[...], 0, 0)
-    for a in range(NAUX):
-        @pl.when(aux == a)
-        def _():
-            off = m_ref[:, (1 - a) * QB:(2 - a) * QB]
-            af[0:QB, 0:QB] = off
-    parts_of(af[0:QB, 0:QB], 0, 1)
-    parts_of(af[0:QB, 0:QB].T, 1, 0)
     msecond.wait_send()
     mcopy(mx, 1, 1 - core, {'orb': orb + 1 - 2 * core}).wait_recv()
     parts_of(mx[...], 1, 1)
@@ -290,23 +291,32 @@
     for a in range(NAUX):
         cols = jnp.concatenate([k[:, o * MP:o * MP + MB] for o in (2 * a, 2 * a + 1)], axis=1)
         for o in range(NORB):
-            kout[a * NORB + o, :, 0:OB] = -cols[o * MP:(o + 1) * MP]
+            kout[o % 2, 2 * a + o // 2, :, 0:OB] = -cols[o * MP:(o + 1) * MP]
     j = jnp.sum(jp[...], axis=1)
     for a in range(NAUX):
-        kout[a * NORB + orb, :, 0:OB] += 2.0 * j[:, a * OB:(a + 1) * OB]
+        kout[core, 2 * a + chip, :, 0:OB] += 2.0 * j[:, a * OB:(a + 1) * OB]
+
+    pair = pltpu.make_async_remote_copy(kout.at[1 - core], kin.at[pl.ds(0, 4)], ks_sem.at[0], kr_sem.at[0],
+                                        device_id=at(6), device_id_type=MESH)
+    pair.start()
+    pair.wait()
+    for b in range(4):
+        kout[core, b] = kout[core, b] + kin[b]
 
     def give(t):
-        return pltpu.make_async_remote_copy(kout.at[index(t)], kin.at[name(t)], ks_sem.at[name(t)], kr_sem.at[name(t)],
+        a, o = peer(t)
+        return pltpu.make_async_remote_copy(kout.at[core, 2 * a + o // 2], kin.at[3 + name(t) // 2],
+                                            ks_sem.at[name(t)], kr_sem.at[name(t)],
                                             device_id=at(t), device_id_type=MESH)
 
-    for t in range(NDEV - 1):
+    for t in (0, 2, 4):
         give(t).start()
-    total = kout[me]
-    for t in range(NDEV - 1):
+    total = kout[core, 2 * aux + chip]
+    for t in (0, 2, 4):
         give(t).wait_recv()
-        total = total + kin[name(t)]
+        total = total + kin[3 + name(t) // 2]
     out_ref[...] = total[0:MB, 0:OB]
-    for t in range(NDEV - 1):
+    for t in (0, 2, 4):
         give(t).wait_send()
 
 
@@ -337,8 +347,8 @@
             pltpu.VMEM((QB, 128), F32),
             pltpu.VMEM((MP, 8, NB), F32),
             pltpu.VMEM((NORB * MP, NORB * MP), F32),
-            pltpu.VMEM((NDEV, MP, 256), F32),
-            pltpu.VMEM((NDEV, MP, 256), F32),
+            pltpu.VMEM((2, 4, MP, 256), F32),
+            pltpu.VMEM((7, MP, 256), F32),
             dma((NBUF,)), dma((NDEV,)), dma((NDEV,)), dma((NDEV,)), dma((NDEV,)),
             dma((2,)), dma((2,)), dma((NDEV,)), dma((NDEV,)),
         ],

time: 157 us -> 154 us (0.981)
  Pallas kernels: 153 us -> 151 us
    pallas_call x1, Pallas kernels: 153 us -> 151 us  [fock(): pl.pallas_call(kernel, name='fock', out_shape=jax.ShapeDtypeStruct((MB, O...]
where the time goes in v11:
time: 154 us
  Pallas kernels  151 us (98%)
  local copies, waits for them, and re-layouts  3.27 us (2%)
    pallas_call x1, Pallas kernels, fock(): pl.pallas_call(kernel, name='fock', out_shape=jax.ShapeDtypeStruct((MB, O...  151 us

profile of v11, /device:TPU:0, one launch (start us, length us, event | category | flops | bytes accessed | tf_op | source)
XLA Modules:
  0.0 154.2 jit_solution(5151058954126759093)
XLA Ops:
  0.0 0.9 constant_dynamic-slice_fusion
  0.9 0.1 copy.4
  1.0 0.6 pad.4.co_ref
  1.6 150.9 %fock.1 = f32[116,232]{1,0:T(8,128)} custom-call(f32[116,464,464]{2,1,0:T(8,128)} %bitcast.b_hbm, f32[40,464]{1,0:T(8,128)} %bitcast.8, f32[120,128]{1,0:T(8,128)} %pad.4.co_ref, f32[464,928]{1,0:T(8,128)} %m_ref.1), custom_call_target="tpu_custom_call" | custom-call | tf_op jit(solution)/shard_map/fock/pallas_call | solution.py:326
  152.5 1.7 %copy.5 = f32[1,116,232]{2,0,1:T(1,128)} copy(f32[1,116,232]{2,1,0:T(8,128)} %bitcast.6) | data formatting | bytes 215296 | tf_op jit(solution)/shard_map/broadcast_in_dim | solution.py:364

commit v12 on v11

--- a/solution.py
+++ b/solution.py
@@ -19,7 +19,7 @@
 MC = 8
 NCH = MP // MC
 TAIL = MB - MC * (NCH - 1)
-SP = 48
+SP = 40
 GR = 4
 NG = MB // GR
 NBUF = 4
@@ -37,10 +37,10 @@
     return a, b, c
 
 
-def kernel(b_hbm, ct_ref, co_ref, m_ref, out_ref,
+def kernel(b_hbm, ct_ref, m_ref, out_ref,
            bbuf, bs, cw, abuf, sbuf, arecv, own, gbuf, gsend, grecv,
            md, mx, ms, af, wb, jp, kacc, kout, kin,
-           bsem, ssem, rsem, gs_sem, gr_sem, ms_sem, mr_sem, ks_sem, kr_sem):
+           bsem, ssem, rsem, gs_sem, gr_sem, ms_sem, mr_sem, ks_sem, kr_sem, co_ref):
     aux, orb = lax.axis_index('aux'), lax.axis_index('orb')
     me = aux * NORB + orb
     core = lax.rem(orb, 2)
@@ -82,6 +82,12 @@
         @pl.when(aux == a)
         def _():
             md[...] = m_ref[:, a * QB:(a + 1) * QB]
+
+    co_ref[...] = jnp.zeros_like(co_ref)
+    for o in range(NORB):
+        @pl.when(orb == o)
+        def _():
+            co_ref[0:MB, 0:NI] = ct_ref[:, o * MB:(o + 1) * MB].T
 
     abuf[...] = jnp.zeros_like(abuf)
     gbuf[...] = jnp.zeros_like(gbuf)
@@ -320,14 +326,14 @@
         give(t).wait_send()
 
 
-def fock(ints, ct, co, metric):
+def fock(ints, ct, metric):
     vmem, hbm = pl.BlockSpec(memory_space=pltpu.VMEM), pl.BlockSpec(memory_space=pl.ANY)
     dma = pltpu.SemaphoreType.DMA
     return pl.pallas_call(
         kernel,
         name='fock',
         out_shape=jax.ShapeDtypeStruct((MB, OB), F32),
-        in_specs=[hbm, vmem, vmem, vmem],
+        in_specs=[hbm, vmem, vmem],
         out_specs=vmem,
         scratch_shapes=[
             pltpu.VMEM((NBUF * GR, QB, NB), F32),
@@ -351,17 +357,15 @@
             pltpu.VMEM((7, MP, 256), F32),
             dma((NBUF,)), dma((NDEV,)), dma((NDEV,)), dma((NDEV,)), dma((NDEV,)),
             dma((2,)), dma((2,)), dma((NDEV,)), dma((NDEV,)),
+            pltpu.VMEM((MP, 128), F32),
         ],
         compiler_params=pltpu.CompilerParams(collective_id=0, has_side_effects=True, vmem_limit_bytes=67043328),
-    )(ints, ct, co, metric)
+    )(ints, ct, metric)
 
 
 def solution(mesh):
     def local_fock(ints, metric, orbitals):
-        orb = lax.axis_index('orb')
-        c = orbitals[0]
-        co = jnp.pad(lax.dynamic_slice_in_dim(c, orb * MB, MB, 0), ((0, MP - MB), (0, 128 - NI)))
-        return fock(jnp.transpose(ints, (1, 0, 2)), c.T, co, metric)[None]
+        return fock(jnp.transpose(ints, (1, 0, 2)), orbitals[0].T, metric)[None]
 
     return jax.shard_map(local_fock, mesh=mesh,
                          in_specs=(P(('sys', 'aux'), 'orb', None), P(('sys', 'aux'), None), P('sys', None, None)),

time: 154 us -> 152 us (0.987)
  local copies, waits for them, and re-layouts: 3.27 us -> 1.67 us
where the time goes in v12:
time: 152 us
  Pallas kernels  151 us (99%)
  local copies, waits for them, and re-layouts  1.67 us (1%)
    pallas_call x1, Pallas kernels, fock(): pl.pallas_call(kernel, name='fock', out_shape=jax.ShapeDtypeStruct((MB, O...  151 us

profile of v12, /device:TPU:0, one launch (start us, length us, event | category | flops | bytes accessed | tf_op | source)
XLA Modules:
  0.0 152.2 jit_solution(7723467810397134697)
XLA Ops:
  0.0 150.6 %fock.1 = f32[116,232]{1,0:T(8,128)} custom-call(f32[116,464,464]{2,1,0:T(8,128)} %bitcast.b_hbm, f32[40,464]{1,0:T(8,128)} %bitcast.6, f32[464,928]{1,0:T(8,128)} %m_ref.1), custom_call_target="tpu_custom_call" | custom-call | tf_op jit(solution)/shard_map/fock/pallas_call | solution.py:332
  150.6 1.7 %copy.4 = f32[1,116,232]{2,0,1:T(1,128)} copy(f32[1,116,232]{2,1,0:T(8,128)} %bitcast.5) | data formatting | bytes 215296 | tf_op jit(solution)/shard_map/broadcast_in_dim | solution.py:368

commit v13 on v12

--- a/solution.py
+++ b/solution.py
@@ -226,9 +226,13 @@
                 fetch(2 * s + x).wait()
         @pl.loop(0, 2 * GR)
         def _(x):
-            for l0, l1 in ((0, 128), (128, 256), (256, 384), (384, NB)):
-                y = bbuf[base * GR + x, :, l0:l1] * wb[:, 0:l1 - l0]
-                jp[2 * GR * s + x, :, l0:l1] = jnp.sum(y.reshape(QB // 8, 8, l1 - l0), axis=0)
+            acc = None
+            for g in range(0, QB, 16):
+                w = wb[g:g + 16, :]
+                w = jnp.concatenate([w, w, w, w[:, 0:NB - 384]], axis=1)
+                y = bbuf[base * GR + x, g:g + 16, :] * w
+                acc = y if acc is None else acc + y
+            jp[2 * GR * s + x] = acc[0:8] + acc[8:16]
 
         for x in range(2):
             @pl.when(2 * s + NBUF + x < NG)

time: 152 us -> 150 us (0.987)
  Pallas kernels: 151 us -> 148 us
    pallas_call x1, Pallas kernels: 151 us -> 148 us  [fock(): pl.pallas_call(kernel, name='fock', out_shape=jax.ShapeDtypeStruct((MB, O...]
where the time goes in v13:
time: 150 us
  Pallas kernels  148 us (99%)
  local copies, waits for them, and re-layouts  1.67 us (1%)
    pallas_call x1, Pallas kernels, fock(): pl.pallas_call(kernel, name='fock', out_shape=jax.ShapeDtypeStruct((MB, O...  148 us

profile of v13, /device:TPU:0, one launch (start us, length us, event | category | flops | bytes accessed | tf_op | source)
XLA Modules:
  0.0 150.2 jit_solution(11474137989397846873)
XLA Ops:
  0.0 148.5 %fock.1 = f32[116,232]{1,0:T(8,128)} custom-call(f32[116,464,464]{2,1,0:T(8,128)} %bitcast.b_hbm, f32[40,464]{1,0:T(8,128)} %bitcast.6, f32[464,928]{1,0:T(8,128)} %m_ref.1), custom_call_target="tpu_custom_call" | custom-call | tf_op jit(solution)/shard_map/fock/pallas_call | solution.py:336
  148.5 1.7 %copy.4 = f32[1,116,232]{2,0,1:T(1,128)} copy(f32[1,116,232]{2,1,0:T(8,128)} %bitcast.5) | data formatting | bytes 215296 | tf_op jit(solution)/shard_map/broadcast_in_dim | solution.py:372

commit v14 on v13

--- a/solution.py
+++ b/solution.py
@@ -325,7 +325,7 @@
     for t in (0, 2, 4):
         give(t).wait_recv()
         total = total + kin[3 + name(t) // 2]
-    out_ref[...] = total[0:MB, 0:OB]
+    out_ref[...] = total[0:MB, 0:OB].reshape(MB, 1, OB)
     for t in (0, 2, 4):
         give(t).wait_send()
 
@@ -336,7 +336,7 @@
     return pl.pallas_call(
         kernel,
         name='fock',
-        out_shape=jax.ShapeDtypeStruct((MB, OB), F32),
+        out_shape=jax.ShapeDtypeStruct((MB, 1, OB), F32),
         in_specs=[hbm, vmem, vmem],
         out_specs=vmem,
         scratch_shapes=[
@@ -369,7 +369,7 @@
 
 def solution(mesh):
     def local_fock(ints, metric, orbitals):
-        return fock(jnp.transpose(ints, (1, 0, 2)), orbitals[0].T, metric)[None]
+        return jnp.transpose(fock(jnp.transpose(ints, (1, 0, 2)), orbitals[0].T, metric), (1, 0, 2))
 
     return jax.shard_map(local_fock, mesh=mesh,
                          in_specs=(P(('sys', 'aux'), 'orb', None), P(('sys', 'aux'), None), P('sys', None, None)),

time: 150 us -> 150 us (level)
    broadcast_in_dim x1 -> x0, local copies, waits for them, and re-layouts: 1.67 us -> none  [local_fock(): return fock(jnp.transpose(ints, (1, 0, 2)), orbitals[0].T, metric)[None]]
    unnamed x0 -> x1, local copies, waits for them, and re-layouts: none -> 1.56 us
where the time goes in v14:
time: 150 us
  Pallas kernels  148 us (99%)
  local copies, waits for them, and re-layouts  1.56 us (1%)
    pallas_call x1, Pallas kernels, fock(): pl.pallas_call(kernel, name='fock', out_shape=jax.ShapeDtypeStruct((MB, 1...  148 us

profile of v14, /device:TPU:0, one launch (start us, length us, event | category | flops | bytes accessed | tf_op | source)
XLA Modules:
  0.0 150.0 jit_solution(11221686981675346978)
XLA Ops:
  0.0 148.5 %fock.1 = f32[116,1,232]{2,1,0:T(1,128)} custom-call(f32[116,464,464]{2,1,0:T(8,128)} %bitcast.b_hbm, f32[40,464]{1,0:T(8,128)} %bitcast.6, f32[464,928]{1,0:T(8,128)} %m_ref.1), custom_call_target="tpu_custom_call" | custom-call | tf_op jit(solution)/shard_map/fock/pallas_call | solution.py:336
  148.5 1.6 %copy.5 = f32[1,116,232]{2,0,1:T(1,128)} copy(f32[1,116,232]{2,0,1:T(1,128)} %bitcast.5) | data formatting | bytes 215296
